TPU v7x, 32 devices: a whole 2x2x4 slice. The times are simulated.
32 devices in a mesh: seq: 8 (over z, x), dp: 4 (over y, core).
Axes of the slice: x: 2, y: 2, z: 4, core: 2. Of those that a mesh axis runs over, the one named last changes fastest.
Arguments:
- conv_input: bfloat16 [4, 2048, 2816], P('dp', 'seq'), may hold values from -6 to 6
- gate_input: bfloat16 [4, 2048, 2560], P('dp', 'seq'), may hold values from -6 to 6
- step_input: float32 [4, 40, 2048], P('dp', None, 'seq'), may hold values from -7.5 to 2048
- filter_taps: float32 [4, 2816], replicated, may hold values from -3 to 3
- filter_bias: float32 [2816], replicated, may hold values from -0.5 to 0.5
- step_bias: float32 [40], replicated, may hold values from -1 to 1
- decay_log: float32 [40], replicated, may hold values from -13 to 3
- skip_gain: float32 [40], replicated, may hold values from 0.5 to 1.5
- norm_weight: float32 [2560], replicated, may hold values from 0.5 to 1.5
- output_weight: bfloat16 [2560, 1280], P('dp'), may hold values from -0.125 to 0.125
- output_grad: bfloat16 [4, 2048, 1280], P('dp', 'seq'), may hold values from -6 to 6
Outputs:
- input_grad: bfloat16 [4, 2048, 2816], P('dp', 'seq')
- gate_grad: bfloat16 [4, 2048, 2560], P('dp', 'seq')
- step_grad: float32 [4, 40, 2048], P('dp', None, 'seq')
- weight_grad: float32 [2560, 1280], P('dp')
- filter_grads: float32 [5, 2816], replicated
- norm_grad: float32 [2560], replicated
- head_grads: float32 [3, 40], replicated
All inputs are finite; a program needn't handle non-finite values.
Results may differ from a plain program's by a relative error of at most 0.0029.
Values may be sent and summed in bfloat16 or wider, within the bound.
A program may use at most 192 MiB of HBM per device.

v0:
```python
import jax
import jax.numpy as jnp
from jax import lax
from jax.sharding import PartitionSpec as P

HEADS = 40
HEAD_DIM = 64
STATE = 128
SPAN = 256
INNER = 2560


PRECISE = lax.Precision.HIGH
MASKED = -1e30
EPSILON = 1e-05


def passed_along(value, axis, steps):
    count = lax.axis_size(axis)
    first, last = (max(0, -steps), min(count, count - steps))
    return lax.ppermute(value, axis, [(source, source + steps) for source in range(first, last)])


def spread(table, axis):
    count = lax.axis_size(axis)
    return lax.all_to_all(
        jnp.broadcast_to(table[None], (count,) + table.shape),
        axis,
        split_axis=0,
        concat_axis=0,
        tiled=True,
    )


def carried(states, decay_table, axis, reverse):
    count = lax.axis_size(axis)
    heads, features, width = states.shape
    pieces = states.reshape(heads, count, features // count, width).transpose(1, 0, 2, 3)
    pieces = lax.all_to_all(pieces, axis, split_axis=0, concat_axis=0, tiled=True)
    running = jnp.zeros(pieces.shape[1:], jnp.float32)
    found = [None] * count
    for at in reversed(range(count)) if reverse else range(count):
        found[at] = running
        running = decay_table[at][:, None, None] * running + pieces[at]
    back = lax.all_to_all(jnp.stack(found), axis, split_axis=0, concat_axis=0, tiled=True)
    return back.transpose(1, 0, 2, 3).reshape(heads, features, width)


def summed_everywhere(parts, axes):
    count = 1
    for axis in axes:
        count = count * lax.axis_size(axis)
    flat = jnp.concatenate([part.reshape(-1) for part in parts])
    chunk = -(-flat.shape[0] // (count * 128)) * 128
    padded = jnp.pad(flat, (0, chunk * count - flat.shape[0])).reshape(count, chunk)
    terms = lax.all_to_all(padded, axes, split_axis=0, concat_axis=0, tiled=True)
    total = lax.all_gather(jnp.sum(terms, axis=0), axes, axis=0, tiled=True)
    results, start = [], 0
    for part in parts:
        results.append(total[start : start + part.size].reshape(part.shape))
        start += part.size
    return results


def prepare(extended, step_rows, filter_taps, filter_bias, step_bias, decay_log):
    width = filter_taps.shape[0]
    length = extended.shape[0] - width + 1
    filtered = filter_bias + filter_taps[0] * extended[0:length]
    for offset in range(1, width):
        filtered = filtered + filter_taps[offset] * extended[offset : offset + length]
    activated = jax.nn.silu(filtered)
    step_sizes = jax.nn.softplus(step_rows + step_bias[:, None])
    decay_rates = step_sizes * (-jnp.exp(decay_log))[:, None]
    blocks = length // SPAN
    cumsums = jnp.cumsum(decay_rates.reshape(HEADS, blocks, SPAN), axis=2)
    values = activated[:, :INNER].reshape(blocks, SPAN, HEADS, HEAD_DIM)
    key_side = activated[:, INNER : INNER + STATE].reshape(blocks, SPAN, STATE)
    scaled = values * step_sizes.reshape(HEADS, blocks, SPAN).transpose(1, 2, 0)[..., None]
    to_end = jnp.exp(cumsums[:, :, -1:] - cumsums)
    block_states = jnp.einsum("hcs,cshp,csn->chpn", to_end, scaled, key_side, precision=PRECISE)
    decays = jnp.exp(cumsums[:, :, -1]).T
    return (activated, cumsums, scaled, block_states, decays)


def finish(
    activated, cumsums, scaled, block_states, decays, entering, skip_gain, gate_rows, norm_weight
):
    blocks = cumsums.shape[1]
    length = blocks * SPAN
    values = activated[:, :INNER].reshape(blocks, SPAN, HEADS, HEAD_DIM)
    key_side = activated[:, INNER : INNER + STATE].reshape(blocks, SPAN, STATE)
    query_side = activated[:, INNER + STATE :].reshape(blocks, SPAN, STATE)
    starting = []
    starting.append(entering)
    starting = jnp.stack(starting)
    scores = jnp.einsum("ctn,csn->cts", query_side, key_side, precision=PRECISE)
    differences = cumsums[:, :, :, None] - cumsums[:, :, None, :]
    causal = jnp.tril(jnp.ones((SPAN, SPAN), dtype=bool))
    weights = scores[None] * jnp.exp(jnp.where(causal, differences, MASKED))
    inside = jnp.einsum("hcts,cshp->cthp", weights, scaled, precision=PRECISE)
    from_state = (
        jnp.einsum("ctn,chpn->cthp", query_side, starting, precision=PRECISE)
        * jnp.exp(cumsums).transpose(1, 2, 0)[..., None]
    )
    result = inside + from_state + skip_gain[:, None] * values
    scanned = result.reshape(length, INNER)
    gated = scanned * jax.nn.silu(gate_rows)
    inverse_rms = lax.rsqrt(jnp.mean(gated * gated, axis=1, keepdims=True) + EPSILON)
    return gated * inverse_rms * norm_weight


def body(
    conv_input,
    gate_input,
    step_input,
    filter_taps,
    filter_bias,
    step_bias,
    decay_log,
    skip_gain,
    norm_weight,
    output_weight,
    output_grad,
):
    kernel_rows = filter_taps.shape[0] - 1
    raw_rows = conv_input[0]
    before = passed_along(raw_rows[-kernel_rows:], "seq", 1)
    extended = jnp.concatenate([before, raw_rows], axis=0).astype(jnp.float32)
    gate_rows = gate_input[0].astype(jnp.float32)
    step_rows = step_input[0]
    cotangent = output_grad[0]
    tokens = cotangent.shape[0]
    primals, pull_first = jax.vjp(
        prepare, extended, step_rows, filter_taps, filter_bias, step_bias, decay_log
    )
    activated, cumsums, scaled, block_states, decays = primals
    decay_table = spread(decays[0], "seq")
    entering = carried(block_states[0], decay_table, "seq", False)
    normed, pull_second = jax.vjp(
        finish,
        activated,
        cumsums,
        scaled,
        block_states,
        decays,
        entering,
        skip_gain,
        gate_rows,
        norm_weight,
    )
    normed_low = normed.astype(jnp.bfloat16)
    groups = lax.axis_size("dp")
    own_rows = output_weight.shape[0]
    everyone = lax.all_gather(cotangent, "dp", axis=0, tiled=True)
    partial_columns = lax.dot_general(
        everyone, output_weight, (((1,), (1,)), ((), ())), preferred_element_type=jnp.float32
    )
    regrouped = partial_columns.reshape(groups, tokens, own_rows)
    normed_grad = lax.all_to_all(regrouped, "dp", split_axis=0, concat_axis=2, tiled=True).reshape(
        tokens, groups * own_rows
    )
    own_columns = lax.all_to_all(normed_low, "dp", split_axis=1, concat_axis=0, tiled=True)
    weight_piece = lax.dot_general(
        own_columns, everyone, (((0,), (0,)), ((), ())), preferred_element_type=jnp.float32
    )
    spans = lax.axis_size("seq")
    weight_terms = lax.all_to_all(
        weight_piece.astype(jnp.bfloat16).reshape(spans, own_rows // spans, -1),
        "seq",
        split_axis=0,
        concat_axis=0,
        tiled=True,
    )
    weight_rows = jnp.sum(weight_terms.astype(jnp.float32), axis=0)
    weight_grad = lax.all_gather(weight_rows, "seq", axis=0, tiled=True)
    second = pull_second(normed_grad)
    (
        grad_activated,
        grad_cumsums,
        grad_scaled,
        grad_states,
        grad_decays,
        grad_entering,
        grad_skip,
        grad_gate,
        grad_norm,
    ) = second
    end_grad = carried(grad_entering, decay_table, "seq", True)
    decay_grad = jnp.sum(end_grad * entering, axis=(1, 2))
    first = pull_first(
        (
            grad_activated,
            grad_cumsums,
            grad_scaled,
            grad_states + end_grad[None],
            grad_decays + decay_grad[None],
        )
    )
    grad_extended, grad_steps, grad_taps, grad_bias, grad_step_bias, grad_decay_log = first
    returned = passed_along(grad_extended[:kernel_rows], "seq", -1)
    own_part = grad_extended[kernel_rows:]
    own_part = jnp.concatenate(
        [own_part[:-kernel_rows], own_part[-kernel_rows:] + returned], axis=0
    )
    filter_part = jnp.concatenate([grad_taps, grad_bias[None]], axis=0)
    head_part = jnp.stack([grad_step_bias, grad_decay_log, grad_skip])
    filter_grads, norm_grad, head_grads = summed_everywhere(
        (filter_part, grad_norm, head_part), ("seq", "dp")
    )
    input_grad = own_part.astype(jnp.bfloat16)[None]
    gate_grad = grad_gate.astype(jnp.bfloat16)[None]
    step_grad = grad_steps[None]
    return (input_grad, gate_grad, step_grad, weight_grad, filter_grads, norm_grad, head_grads)


def solution(mesh):
    return jax.shard_map(
        body,
        mesh=mesh,
        in_specs=(
            P("dp", "seq", None),
            P("dp", "seq", None),
            P("dp", None, "seq"),
            P(),
            P(),
            P(),
            P(),
            P(),
            P(),
            P("dp", None),
            P("dp", "seq", None),
        ),
        out_specs=(
            P("dp", "seq", None),
            P("dp", "seq", None),
            P("dp", None, "seq"),
            P("dp", None),
            P(),
            P(),
            P(),
        ),
        check_vma=False,
    )
```

profile of v0, /device:TPU:0, one launch (start us, length us, event | category | flops | bytes accessed | tf_op | source)
XLA Modules:
  0.0 410.9 jit_solution(12304909783855509701)
XLA Ops:
  8.1 4.9 %collective-permute-start = (bf16[3,2816]{1,0:T(4,128)(2,1)S(1)}, bf16[3,2816]{1,0:T(4,128)(2,1)S(1)}, u32[]{:S(2)}, u32[]{:S(2)}) collective-permute-start(bf16[3,2816]{1,0:T(4,128)(2,1)S(1)} %slice_bitcast_fusion), channel_id=1, source_target_pairs={{0,4},{4,8},{8,12},{12,16},{16,20},{20,24},{24,28},{1,5},{5,9},{9,... | collective-permute-start | bytes 50696 | tf_op jit(solution)/shard_map/ppermute | solution.py:21
  16.9 4.9 %all-to-all-start.1 = ((f32[8,1,40]{2,1,0:T(1,128)}), f32[8,1,40]{2,1,0:T(1,128)S(1)}, u32[]{:S(2)}, u32[]{:S(2)}) async-start(f32[8,1,40]{2,1,0:T(1,128)} %broadcast_in_dim.32), calls=%async_computation.1 | async-start | bytes 8192 | tf_op jit(solution)/shard_map/all_to_all | solution.py:26
  26.6 3.0 fusion.19
  33.1 3.2 copy.219
  36.4 3.0 fusion.64
  41.1 6.0 %all-to-all-start.2 = ((f32[8,40,8,128]{3,2,1,0:T(8,128)}), f32[8,40,8,128]{3,2,1,0:T(8,128)S(1)}, u32[]{:S(2)}, u32[]{:S(2)}) async-start(f32[8,40,8,128]{3,2,1,0:T(8,128)} %copy.225), calls=%async_computation.2 | async-start | bytes 2621440 | tf_op jit(solution)/shard_map/all_to_all | solution.py:39
  49.9 28.0 %all-to-all-done.2 = f32[8,40,8,128]{3,2,1,0:T(8,128)S(1)} async-done(((f32[8,40,8,128]{3,2,1,0:T(8,128)}), f32[8,40,8,128]{3,2,1,0:T(8,128)S(1)}, u32[]{:S(2)}, u32[]{:S(2)}) %all-to-all-start.2) | async-done | bytes 1310752 | tf_op jit(solution)/shard_map/all_to_all | solution.py:39
  83.4 3.6 all-to-all-start.3
  87.1 5.5 %fusion.44 = f32[1024,640]{1,0:T(8,128)} fusion(bf16[640,1280]{1,0:T(8,128)(2,1)S(1)} %copy-done, bf16[1,1024,1280]{2,1,0:T(8,128)(2,1)} %all-gather.7.cloned.1.call-done), kind=kOutput, calls=%fused_computation.67 | convolution fusion | flops 1677721600 | bytes 6881280 | tf_op jit(solution)/shard_map/dot_general | solution.py:155
  92.6 25.8 %all-to-all-done.3 = f32[8,40,8,128]{3,2,1,0:T(8,128)S(1)} async-done(((f32[8,40,8,128]{3,2,1,0:T(8,128)}), f32[8,40,8,128]{3,2,1,0:T(8,128)S(1)}, u32[]{:S(2)}, u32[]{:S(2)}) %all-to-all-start.3) | async-done | bytes 1310752 | tf_op jit(solution)/shard_map/all_to_all | solution.py:45
  119.5 4.1 %all-to-all-start = ((f32[4,256,640]{2,1,0:T(8,128)}), f32[4,256,640]{2,1,0:T(8,128)S(1)}, u32[]{:S(2)}, u32[]{:S(2)}) async-start(f32[4,256,640]{2,1,0:T(8,128)} %bitcast.338), calls=%async_computation | async-start | bytes 5242880 | tf_op jit(solution)/shard_map/all_to_all | solution.py:159
  123.8 2.4 copy.229
  126.2 3.2 convert_element_type.89
  130.7 3.7 fusion.74
  134.4 20.4 %all-to-all-done = f32[4,256,640]{2,1,0:T(8,128)S(1)} async-done(((f32[4,256,640]{2,1,0:T(8,128)}), f32[4,256,640]{2,1,0:T(8,128)S(1)}, u32[]{:S(2)}, u32[]{:S(2)}) %all-to-all-start) | async-done | bytes 2621472 | tf_op jit(solution)/shard_map/all_to_all | solution.py:159
  154.8 2.5 copy.218
  157.3 10.1 %multiply_reduce_fusion.9 = (f32[256]{0:T(256)S(1)}, f32[256]{0:T(256)S(1)}, f32[1,256,40,64]{1,3,2,0:T(8,128)S(1)}) fusion(f32[1,256,40,64]{1,3,2,0:T(8,128)} %bitcast.317, f32[1,256,40,64]{1,3,2,0:T(8,128)} %bitcast.329, f32[40,64]{1,0:T(8,128)S(1)} %mul.692, f32[1,256,40,64]{1,3,2,0:T(8,128)} %bitcast.323, f32[40]{0:T(128)S(1)} %copy-done.51, ...), kind=kOutput, calls=%fused_computation.74 | convolution fusion | flops 1024327168 | bytes 16191648 | tf_op jit(solution)/shard_map/jvp(hcts,cshp->cthp)/dot_general | solution.py:100
  169.4 4.3 %all-to-all-start.6 = ((bf16[256,4,640]{0,2,1:T(8,128)(2,1)}), bf16[256,4,640]{0,2,1:T(8,128)(2,1)}, u32[]{:S(2)}, u32[]{:S(2)}) async-start(bf16[256,4,640]{0,2,1:T(8,128)(2,1)} %multiply_convert_fusion), calls=%async_computation.6 | async-start | bytes 2621440 | tf_op jit(solution)/shard_map/all_to_all | solution.py:162
  173.7 4.2 %broadcast_multiply_fusion.5 = (f32[1,256,40,64]{1,3,2,0:T(8,128)}, f32[1,256,40,64]{1,3,2,0:T(8,128)S(1)}) fusion(f32[40]{0:T(128)S(1)} %copy-done.51, f32[256]{0:T(256)S(1)} %get-tuple-element.107, f32[1,256,40,64]{1,3,2,0:T(8,128)S(1)} %get-tuple-element.108, f32[1,256,40,64]{1,3,2,0:T(8,128)} %bitcast.318, f32[256]{0:T(256)S(1)} %get-tuple-element.106, ...), kind=kLoop, calls=%fused_computation.104 | loop fusion | flops 7864320 | bytes 13119648 | tf_op jit(solution)/shard_map/transpose(jvp())/mul | solution.py:105
  182.7 8.2 %all-to-all-done.6 = bf16[256,4,640]{0,2,1:T(8,128)(2,1)} async-done(((bf16[256,4,640]{0,2,1:T(8,128)(2,1)}), bf16[256,4,640]{0,2,1:T(8,128)(2,1)}, u32[]{:S(2)}, u32[]{:S(2)}) %all-to-all-start.6) | async-done | bytes 1310752 | tf_op jit(solution)/shard_map/all_to_all | solution.py:162
  191.0 4.3 %all-to-all-start.4 = ((f32[8,40,8,128]{3,2,1,0:T(8,128)}), f32[8,40,8,128]{3,2,1,0:T(8,128)}, u32[]{:S(2)}, u32[]{:S(2)}) async-start(f32[8,40,8,128]{3,2,1,0:T(8,128)} %copy.232), calls=%async_computation.4 | async-start | bytes 2621440 | tf_op jit(solution)/shard_map/all_to_all | solution.py:39
  195.3 3.2 copy.247
  198.5 2.4 copy.245
  200.9 5.3 %convolution_convert_fusion = bf16[640,1280]{1,0:T(8,128)(2,1)} fusion(bf16[1024,640]{1,0:T(8,128)(2,1)} %bitcast.342, bf16[1,1024,1280]{2,1,0:T(8,128)(2,1)} %all-gather.7.cloned.1.call-done), kind=kOutput, calls=%fused_computation.24 | convolution fusion | flops 1678540800 | bytes 5570560 | tf_op jit(solution)/shard_map/dot_general | solution.py:163
  206.2 20.4 %all-to-all-done.4 = f32[8,40,8,128]{3,2,1,0:T(8,128)} async-done(((f32[8,40,8,128]{3,2,1,0:T(8,128)}), f32[8,40,8,128]{3,2,1,0:T(8,128)}, u32[]{:S(2)}, u32[]{:S(2)}) %all-to-all-start.4) | async-done | bytes 1310752 | tf_op jit(solution)/shard_map/all_to_all | solution.py:39
  226.6 4.5 %all-to-all-start.7 = ((bf16[8,80,1280]{2,1,0:T(8,128)(2,1)}), bf16[8,80,1280]{2,1,0:T(8,128)(2,1)}, u32[]{:S(2)}, u32[]{:S(2)}) async-start(bf16[8,80,1280]{2,1,0:T(8,128)(2,1)} %bitcast.340), calls=%async_computation.7 | async-start | bytes 3276800 | tf_op jit(solution)/shard_map/all_to_all | solution.py:167
  231.1 4.3 %fusion.24 = bf16[1,256,2560]{1,2,0:T(8,128)(2,1)} fusion(f32[1,256,4,640]{1,3,2,0:T(8,128)} %copy.218, f32[1,256,40,64]{1,3,2,0:T(8,128)S(1)} %get-tuple-element.108, f32[256]{0:T(256)S(1)} %get-tuple-element.107, f32[256]{0:T(256)S(1)} %get-tuple-element.106, f32[2560]{0:T(1024)S(1)} %copy-done.25, bf16[1,256,2560]{1,2,0:T(8,128)(2,1)} %copy.229), kind=kLoop, calls=%fused_computation.40 | loop fusion | flops 12451840 | bytes 7876608 | tf_op jit(solution)/shard_map/convert_element_type | solution.py:211
  235.4 2.4 copy.251
  237.9 4.0 fusion.27
  242.6 3.2 copy.231
  245.9 2.4 fusion.99
  256.0 13.1 %all-to-all-done.7 = bf16[8,80,1280]{2,1,0:T(8,128)(2,1)} async-done(((bf16[8,80,1280]{2,1,0:T(8,128)(2,1)}), bf16[8,80,1280]{2,1,0:T(8,128)(2,1)}, u32[]{:S(2)}, u32[]{:S(2)}) %all-to-all-start.7) | async-done | bytes 1638432 | tf_op jit(solution)/shard_map/all_to_all | solution.py:167
  269.1 4.3 %all-to-all-start.5 = ((f32[8,40,8,128]{3,2,1,0:T(8,128)}), f32[8,40,8,128]{3,2,1,0:T(8,128)}, u32[]{:S(2)}, u32[]{:S(2)}) async-start(f32[8,40,8,128]{3,2,1,0:T(8,128)} %broadcast_dynamic-update-slice_fusion), calls=%async_computation.5 | async-start | bytes 2621440 | tf_op jit(solution)/shard_map/all_to_all | solution.py:45
  273.5 13.1 %fusion.6 = (f32[40,256]{1,0:T(8,128)}, f32[40,256]{1,0:T(8,128)S(1)}, f32[256,256]{1,0:T(8,128)S(1)}) fusion(f32[40,256]{1,0:T(8,128)} %get-tuple-element.88, f32[256,256]{1,0:T(8,128)S(1)} %copy-done.17, pred[256,256]{1,0:T(8,128)(4,1)} %copy-done.26, f32[256,40,64]{0,2,1:T(8,128)} %bitcast.325, f32[256,40]{0,1:T(8,128)S(1)} %fusion.124, ...), kind=kOutput, calls=%fused_computation.7 | convolution fusion | flops 1030795264 | bytes 5996544 | tf_op jit(solution)/shard_map/transpose(jvp(hcts,cshp->cthp))/dot_general | solution.py:100
  288.9 2.2 copy.248
  291.0 4.4 %multiply_reduce_fusion.6 = f32[4,640]{1,0:T(4,128)S(1)} fusion(f32[1,256,4,640]{3,1,2,0:T(8,128)} %copy.248, f32[1,256,4,640]{3,1,2,0:T(8,128)} %copy.247, f32[256]{0:T(256)S(1)} %copy-done.31, f32[4,256,640]{2,1,0:T(8,128)} %copy-done.6), kind=kLoop, calls=%fused_computation.70 | loop fusion | flops 5240320 | bytes 7875584 | tf_op jit(solution)/shard_map/transpose(jvp())/reduce_sum | solution.py:109
  297.4 3.5 fusion.93
  302.1 2.6 convert_reduce_fusion
  308.1 3.3 fusion.34
  311.5 7.5 %multiply_reduce_fusion.5 = (f32[40]{0:T(128)}, f32[256,40]{0,1:T(8,128)}, f32[1,256,40,64]{1,3,2,0:T(8,128)}) fusion(f32[1,256,40,64]{1,3,2,0:T(8,128)S(1)} %copy-done.9, f32[1,256,40,64]{1,3,2,0:T(8,128)S(1)} %bitcast.327, f32[256,40]{0,1:T(8,128)S(1)} %fusion.124, f32[256,40]{0,1:T(8,128)S(1)} %get-tuple-element.87, ...), kind=kOutput, calls=%fused_computation.69 | convolution fusion | flops 1019074560 | bytes 10977440 | tf_op jit(solution)/shard_map/transpose(jvp(hcts,cshp->cthp))/dot_general | solution.py:100
  318.9 3.3 copy.235
  322.2 3.7 fusion.88
  325.9 5.4 %multiply_reduce_fusion.4 = (f32[2816]{0:T(1024)S(1)}, f32[2816]{0:T(1024)S(1)}, f32[2816]{0:T(1024)S(1)}, f32[2816]{0:T(1024)S(1)}, f32[2816]{0:T(1024)}, /*index=5*/f32[256,2816]{1,0:T(8,128)S(1)}) fusion(f32[259,2816]{1,0:T(8,128)S(1)} %copy-done.3, f32[256,2816]{1,0:T(8,128)} %get-tuple-element.90, f32[256,2560]{1,0:T(8,128)} %copy.235, ...), kind=kLoop, calls=%fused_computation.32 | loop fusion | flops 15845632 | bytes 22993920 | tf_op jit(solution)/shard_map/transpose(jvp())/reduce_sum | solution.py:70
  333.4 2.5 reduce-window.16
  343.5 5.1 %all-to-all-start.8 = ((f32[32,1,640]{2,1,0:T(1,128)}), f32[32,1,640]{2,1,0:T(1,128)S(1)}, u32[]{:S(2)}, u32[]{:S(2)}) async-start(f32[32,1,640]{2,1,0:T(1,128)} %bitcast.102), calls=%async_computation.8 | async-start | bytes 163840 | tf_op jit(solution)/shard_map/all_to_all | solution.py:56
  352.8 3.8 collective-permute-done.1
  357.9 40.0 %all-gather.1 = f32[32,1,640]{2,1,0:T(1,128)S(1)} all-gather(f32[1,1,640]{2,1,0:T(1,128)S(1)} %reshape.1035), channel_id=1, replica_groups=mesh['seq'=8,'dp'=4] {'seq','dp'}, dimensions={0}, use_global_device_ids=true | all-gather | bytes 84480 | tf_op jit(solution)/shard_map/all_gather | solution.py:57
  400.0 3.8 copy.324
  (212 shorter events, 66.9 us)
Async XLA Ops:
  7.2 79.9 %copy-start = (bf16[640,1280]{1,0:T(8,128)(2,1)S(1)}, bf16[640,1280]{1,0:T(8,128)(2,1)}, u32[]{:S(2)}) copy-start(bf16[640,1280]{1,0:T(8,128)(2,1)} %param.20) | copy-start | bytes 4915204
  8.1 16.8 %collective-permute-start = (bf16[3,2816]{1,0:T(4,128)(2,1)S(1)}, bf16[3,2816]{1,0:T(4,128)(2,1)S(1)}, u32[]{:S(2)}, u32[]{:S(2)}) collective-permute-start(bf16[3,2816]{1,0:T(4,128)(2,1)S(1)} %slice_bitcast_fusion), channel_id=1, source_target_pairs={{0,4},{4,8},{8,12},{12,16},{16,20},{20,24},{24,28},{1,5},{5,9},{9,... | collective-permute-start | bytes 50696 | tf_op jit(solution)/shard_map/ppermute | solution.py:21
  16.2 13.4 %copy-start.20 = (f32[40,1,256]{0,2,1:T(8,128)}, f32[40,1,256]{0,2,1:T(8,128)S(1)}, u32[]{:S(2)}) copy-start(f32[40,1,256]{0,2,1:T(8,128)S(1)} %get-tuple-element.97) | copy-start | bytes 122884
  16.2 10.4 %copy-start.33 = (f32[2816]{0:T(1024)S(1)}, f32[2816]{0:T(1024)}, u32[]{:S(2)}) copy-start(f32[2816]{0:T(1024)} %param.15) | copy-start | bytes 33796
  16.9 23.6 %all-to-all-start.1 = ((f32[8,1,40]{2,1,0:T(1,128)}), f32[8,1,40]{2,1,0:T(1,128)S(1)}, u32[]{:S(2)}, u32[]{:S(2)}) async-start(f32[8,1,40]{2,1,0:T(1,128)} %broadcast_in_dim.32), calls=%async_computation.1 | async-start | bytes 8192 | tf_op jit(solution)/shard_map/all_to_all | solution.py:26
  24.9 4.7 %copy-start.21 = (f32[2816]{0:T(1024)}, f32[2816]{0:T(1024)S(1)}, u32[]{:S(2)}) copy-start(f32[2816]{0:T(1024)S(1)} %get-tuple-element.70) | copy-start | bytes 33796
  24.9 4.7 %copy-start.22 = (f32[2816]{0:T(1024)}, f32[2816]{0:T(1024)S(1)}, u32[]{:S(2)}) copy-start(f32[2816]{0:T(1024)S(1)} %get-tuple-element.71) | copy-start | bytes 33796
  24.9 4.7 %copy-start.23 = (f32[2816]{0:T(1024)}, f32[2816]{0:T(1024)S(1)}, u32[]{:S(2)}) copy-start(f32[2816]{0:T(1024)S(1)} %get-tuple-element.72) | copy-start | bytes 33796
  24.9 4.7 %copy-start.24 = (f32[2816]{0:T(1024)}, f32[2816]{0:T(1024)S(1)}, u32[]{:S(2)}) copy-start(f32[2816]{0:T(1024)S(1)} %get-tuple-element.73) | copy-start | bytes 33796
  41.1 36.8 %all-to-all-start.2 = ((f32[8,40,8,128]{3,2,1,0:T(8,128)}), f32[8,40,8,128]{3,2,1,0:T(8,128)S(1)}, u32[]{:S(2)}, u32[]{:S(2)}) async-start(f32[8,40,8,128]{3,2,1,0:T(8,128)} %copy.225), calls=%async_computation.2 | async-start | bytes 2621440 | tf_op jit(solution)/shard_map/all_to_all | solution.py:39
  47.1 40.0 %all-gather.7.cloned.1.call-start = ((), (), s32[]{:S(2)}) async-start(), calls=%async_computation.10 | async-start | bytes 3276800 | tf_op jit(solution)/shard_map/all_gather | solution.py:154
  49.8 33.6 %copy-start.34 = (f32[40]{0:T(128)}, f32[40]{0:T(128)S(1)}, u32[]{:S(2)}) copy-start(f32[40]{0:T(128)S(1)} %get-tuple-element.100) | copy-start | bytes 484
  49.8 33.6 %copy-start.37 = (f32[40]{0:T(128)}, f32[40]{0:T(128)S(1)}, u32[]{:S(2)}) copy-start(f32[40]{0:T(128)S(1)} %get-tuple-element.102) | copy-start | bytes 484
  49.8 33.6 %copy-start.39 = (f32[40]{0:T(128)}, f32[40]{0:T(128)S(1)}, u32[]{:S(2)}) copy-start(f32[40]{0:T(128)S(1)} %get-tuple-element.101) | copy-start | bytes 484
  49.8 33.6 %copy-start.41 = (f32[40]{0:T(128)}, f32[40]{0:T(128)S(1)}, u32[]{:S(2)}) copy-start(f32[40]{0:T(128)S(1)} %get-tuple-element.103) | copy-start | bytes 484
  49.9 33.6 %copy-start.46 = (f32[40]{0:T(128)}, f32[40]{0:T(128)S(1)}, u32[]{:S(2)}) copy-start(f32[40]{0:T(128)S(1)} %get-tuple-element.99) | copy-start | bytes 484
  49.9 33.6 %copy-start.48 = (f32[40]{0:T(128)}, f32[40]{0:T(128)S(1)}, u32[]{:S(2)}) copy-start(f32[40]{0:T(128)S(1)} %get-tuple-element.104) | copy-start | bytes 484
  83.4 35.0 %all-to-all-start.3 = ((f32[8,40,8,128]{3,2,1,0:T(8,128)}), f32[8,40,8,128]{3,2,1,0:T(8,128)S(1)}, u32[]{:S(2)}, u32[]{:S(2)}) async-start(f32[8,40,8,128]{3,2,1,0:T(8,128)} %fusion.100), calls=%async_computation.3 | async-start | bytes 2621440 | tf_op jit(solution)/shard_map/all_to_all | solution.py:45
  118.4 5.2 %copy-start.25 = (f32[2560]{0:T(1024)S(1)}, f32[2560]{0:T(1024)}, u32[]{:S(2)}) copy-start(f32[2560]{0:T(1024)} %param.19) | copy-start | bytes 30724
  119.5 35.4 %all-to-all-start = ((f32[4,256,640]{2,1,0:T(8,128)}), f32[4,256,640]{2,1,0:T(8,128)S(1)}, u32[]{:S(2)}, u32[]{:S(2)}) async-start(f32[4,256,640]{2,1,0:T(8,128)} %bitcast.338), calls=%async_computation | async-start | bytes 5242880 | tf_op jit(solution)/shard_map/all_to_all | solution.py:159
  123.8 54.2 %copy-start.14 = (f32[256,40]{0,1:T(8,128)}, f32[256,40]{0,1:T(8,128)S(1)}, u32[]{:S(2)}) copy-start(f32[256,40]{0,1:T(8,128)S(1)} %copy.227) | copy-start | bytes 122884
  126.2 4.5 %copy-start.11 = (f32[8,40,8,128]{3,2,1,0:T(8,128)S(1)}, f32[8,40,8,128]{3,2,1,0:T(8,128)}, u32[]{:S(2)}) copy-start(f32[8,40,8,128]{3,2,1,0:T(8,128)} %copy-done.10) | copy-start | bytes 3932164
  129.4 27.9 %copy-start.26 = (pred[256,256]{1,0:T(8,128)(4,1)}, pred[256,256]{1,0:T(8,128)(4,1)S(1)}, u32[]{:S(2)}) copy-start(pred[256,256]{1,0:T(8,128)(4,1)S(1)} %iota_compare_fusion) | copy-start | bytes 196612
  130.7 26.6 %copy-start.16 = (f32[256,256]{1,0:T(8,128)}, f32[256,256]{1,0:T(8,128)S(1)}, u32[]{:S(2)}) copy-start(f32[256,256]{1,0:T(8,128)S(1)} %fusion.115) | copy-start | bytes 786436
  157.3 10.1 %copy-start.4 = (f32[1,256,2560]{1,2,0:T(8,128)S(1)}, f32[1,256,2560]{1,2,0:T(8,128)}, u32[]{:S(2)}) copy-start(f32[1,256,2560]{1,2,0:T(8,128)} %convert_element_type.89) | copy-start | bytes 7864324
  167.4 70.4 %copy-start.30 = (f32[256]{0:T(256)}, f32[256]{0:T(256)S(1)}, u32[]{:S(2)}) copy-start(f32[256]{0:T(256)S(1)} %get-tuple-element.106) | copy-start | bytes 3076
  169.4 21.6 %all-to-all-start.6 = ((bf16[256,4,640]{0,2,1:T(8,128)(2,1)}), bf16[256,4,640]{0,2,1:T(8,128)(2,1)}, u32[]{:S(2)}, u32[]{:S(2)}) async-start(bf16[256,4,640]{0,2,1:T(8,128)(2,1)} %multiply_convert_fusion), calls=%async_computation.6 | async-start | bytes 2621440 | tf_op jit(solution)/shard_map/all_to_all | solution.py:162
  191.0 35.6 %all-to-all-start.4 = ((f32[8,40,8,128]{3,2,1,0:T(8,128)}), f32[8,40,8,128]{3,2,1,0:T(8,128)}, u32[]{:S(2)}, u32[]{:S(2)}) async-start(f32[8,40,8,128]{3,2,1,0:T(8,128)} %copy.232), calls=%async_computation.4 | async-start | bytes 2621440 | tf_op jit(solution)/shard_map/all_to_all | solution.py:39
  226.6 42.5 %all-to-all-start.7 = ((bf16[8,80,1280]{2,1,0:T(8,128)(2,1)}), bf16[8,80,1280]{2,1,0:T(8,128)(2,1)}, u32[]{:S(2)}, u32[]{:S(2)}) async-start(bf16[8,80,1280]{2,1,0:T(8,128)(2,1)} %bitcast.340), calls=%async_computation.7 | async-start | bytes 3276800 | tf_op jit(solution)/shard_map/all_to_all | solution.py:167
  242.6 3.3 copy-start.44
  245.8 5.5 %copy-start.36 = (f32[40]{0:T(128)S(1)}, f32[40]{0:T(128)}, u32[]{:S(2)}) copy-start(f32[40]{0:T(128)} %copy-done.34) | copy-start | bytes 484
  245.8 7.8 %copy-start.45 = (f32[40]{0:T(128)S(1)}, f32[40]{0:T(128)}, u32[]{:S(2)}) copy-start(f32[40]{0:T(128)} %get-tuple-element.98) | copy-start | bytes 484
  248.3 25.2 %copy-start.17 = (f32[256,256]{1,0:T(8,128)S(1)}, f32[256,256]{1,0:T(8,128)}, u32[]{:S(2)}) copy-start(f32[256,256]{1,0:T(8,128)} %copy-done.16) | copy-start | bytes 786436
  269.1 35.6 %all-to-all-start.5 = ((f32[8,40,8,128]{3,2,1,0:T(8,128)}), f32[8,40,8,128]{3,2,1,0:T(8,128)}, u32[]{:S(2)}, u32[]{:S(2)}) async-start(f32[8,40,8,128]{3,2,1,0:T(8,128)} %broadcast_dynamic-update-slice_fusion), calls=%async_computation.5 | async-start | bytes 2621440 | tf_op jit(solution)/shard_map/all_to_all | solution.py:45
  273.4 126.6 %all-gather.5.cloned.1.call-start = ((), (), s32[]{:S(2)}) async-start(), calls=%async_computation.9 | async-start | bytes 3686400 | tf_op jit(solution)/shard_map/all_gather | solution.py:175
  291.0 6.3 %copy-start.8 = (f32[1,256,40,64]{1,3,2,0:T(8,128)S(1)}, f32[1,256,40,64]{1,3,2,0:T(8,128)}, u32[]{:S(2)}) copy-start(f32[1,256,40,64]{1,3,2,0:T(8,128)} %copy-done.7) | copy-start | bytes 7864324
  291.0 6.3 %copy-start.15 = (f32[256,40]{0,1:T(8,128)S(1)}, f32[256,40]{0,1:T(8,128)}, u32[]{:S(2)}) copy-start(f32[256,40]{0,1:T(8,128)} %copy-done.14) | copy-start | bytes 122884
  302.1 6.0 %copy-start.5 = (f32[256,2560]{0,1:T(8,128)S(1)}, f32[256,2560]{0,1:T(8,128)}, u32[]{:S(2)}) copy-start(f32[256,2560]{0,1:T(8,128)} %copy.219) | copy-start | bytes 7864324
  308.1 3.4 copy-start.9
  308.1 3.4 copy-start.18
  308.1 3.4 copy-start.27
  308.1 3.3 copy-start.29
  322.2 3.7 copy-start.3
  325.9 5.5 %copy-start.19 = (f32[256,40]{0,1:T(8,128)S(1)}, f32[256,40]{0,1:T(8,128)}, u32[]{:S(2)}) copy-start(f32[256,40]{0,1:T(8,128)} %get-tuple-element.109) | copy-start | bytes 122884
  325.9 11.2 %copy-start.13 = (f32[1,40,256]{2,1,0:T(8,128)S(1)}, f32[1,40,256]{2,1,0:T(8,128)}, u32[]{:S(2)}) copy-start(f32[1,40,256]{2,1,0:T(8,128)} %param.13) | copy-start | bytes 122884
  343.5 14.4 %all-to-all-start.8 = ((f32[32,1,640]{2,1,0:T(1,128)}), f32[32,1,640]{2,1,0:T(1,128)S(1)}, u32[]{:S(2)}, u32[]{:S(2)}) async-start(f32[32,1,640]{2,1,0:T(1,128)} %bitcast.102), calls=%async_computation.8 | async-start | bytes 163840 | tf_op jit(solution)/shard_map/all_to_all | solution.py:56
  350.3 6.3 %collective-permute-start.1 = (f32[3,2816]{1,0:T(4,128)S(1)}, f32[3,2816]{1,0:T(4,128)S(1)}, u32[]{:S(2)}, u32[]{:S(2)}) collective-permute-start(f32[3,2816]{1,0:T(4,128)S(1)} %pad_add_fusion.1), channel_id=1, source_target_pairs={{4,0},{8,4},{12,8},{16,12},{20,16},{24,20},{28,24},{5,1},{9,5},{13... | collective-permute-start | bytes 101384 | tf_op jit(solution)/shard_map/ppermute | solution.py:21
  399.4 4.5 %copy-start.1 = (bf16[640,1280]{1,0:T(8,128)(2,1)S(1)}, bf16[640,1280]{1,0:T(8,128)(2,1)}, u32[]{:S(2)}) copy-start(bf16[640,1280]{1,0:T(8,128)(2,1)} %param.20) | copy-start | bytes 4915204
  (17 other events, 39.9 us)
Sparse Core Ops, SparseCore 0:
  49.4 26.9 all-gather.6
  304.8 62.9 all-gather.4
where the time goes:
time: 418 us; the launch traced here: 411 us
  waiting for transfers between devices  120 us (29%)
  other arithmetic  69.1 us (17%)
  matrix products  64.5 us (15%)
  local copies, waits for them, and re-layouts  54.6 us (13%)
  starting transfers between devices  47.2 us (11%)
  blocking collectives  40 us (10%)
  between operations  15.1 us (4%)
    all_to_all x2, waiting for transfers between devices, carried(): lax.all_to_all(pieces, axis, split_axis=0, concat_axis=0, tiled=True)  48.4 us
    all_gather x1, blocking collectives, summed_everywhere(): total = lax.all_gather(jnp.sum(terms, axis=0), axes, axis=0, tiled=True)  40 us
    dot_general x3, matrix products, finish(): inside = jnp.einsum('hcts,cshp->cthp', weights, scaled, precision=PRECISE)  30.7 us
    all_to_all x2, waiting for transfers between devices, carried(): lax.all_to_all(jnp.stack(found), axis, split_axis=0, concat_axis=0, tiled...  25.8 us
    all_to_all x1, waiting for transfers between devices, body(): lax.all_to_all(regrouped, 'dp', split_axis=0, concat_axis=2, tiled=True)  20.4 us
    unnamed x113, local copies, waits for them, and re-layouts  17.5 us
    all_to_all x1, waiting for transfers between devices, body(): lax.all_to_all(weight_piece.astype(jnp.bfloat16).reshape(spans, own_rows...  13.1 us
    unnamed x10, other arithmetic  12.2 us
  transfers between devices with their start and end apart: 13, of which 7 were waited for; matrix products, arithmetic and copies ran while one was open for 40% of the time, Pallas kernels for 0%

commit v1 on v0

v1 whole, which is shorter than its diff:
```python
import functools

import jax
import jax.numpy as jnp
from jax import lax
from jax.experimental import pallas as pl
from jax.experimental.pallas import tpu as pltpu
from jax.sharding import PartitionSpec as P

F32 = jnp.float32
BF16 = jnp.bfloat16
EPSILON = 1e-05
LOG2E = 1.4426950408889634
LANES = 128
HEAD_DIM = 64
GROUP = 2
MESH = pl.DeviceIdType.MESH
NN = (((1,), (0,)), ((), ()))
NT = (((1,), (1,)), ((), ()))
TN = (((0,), (0,)), ((), ()))


def dot(a, b, dims=NN):
    return lax.dot_general(a, b, dims, preferred_element_type=F32)


def rounded_high(a):
    scaled = a * 65537.0
    return scaled - (scaled - a)


def split2(a):
    high = rounded_high(a)
    return high.astype(BF16), (a - high).astype(BF16)


def split3(a):
    high = rounded_high(a)
    rest = a - high
    middle = rounded_high(rest)
    return high.astype(BF16), middle.astype(BF16), (rest - middle).astype(BF16)


def dot3(a, b, dims=NN):
    return dot(a[0], b[0], dims) + (dot(a[0], b[1], dims) + dot(a[1], b[0], dims))


def chunk_of(index):
    return pl.ds(pl.multiple_of(index * LANES, LANES), LANES)


def iota(shape, dim):
    return lax.broadcasted_iota(jnp.int32, shape, dim)


def low_half(shape):
    return iota(shape, 1) < HEAD_DIM


def head_rows(index):
    shape = (LANES, LANES)
    wanted = 2 * index + jnp.where(low_half(shape), 0, 1)
    return jnp.where(iota(shape, 0) == wanted, 1.0, 0.0).astype(BF16)


def sigmoid(a):
    return 1.0 / (1.0 + jnp.exp(-a))


def transposed(rows):
    heads, tokens = rows.shape
    padded = jnp.concatenate([rows, jnp.zeros((LANES - heads, tokens), F32)], axis=0)
    return padded.T


def step_phase(step, step_bias, decay_log, cum_rows, cum_cols, dt_cols):
    shifted = step[...] + step_bias[...]
    sizes = jnp.maximum(shifted, 0.0) + jnp.log1p(jnp.exp(-jnp.abs(shifted)))
    rates = -jnp.exp(decay_log[...]) * sizes
    tokens = rates.shape[1]
    shape = (tokens, tokens)
    before = jnp.where(iota(shape, 0) <= iota(shape, 1), 1.0, 0.0).astype(BF16)
    high, middle, low = split3(rates)
    cumulative = (dot(high, before) + (dot(middle, before) + dot(low, before))) * LOG2E
    for head in range(rates.shape[0]):
        cum_rows[head] = cumulative[head : head + 1]
    cum_cols[...] = transposed(cumulative)
    dt_cols[...] = transposed(sizes)


def expand_phase(cum_cols, dt_cols, cum_wide, dt_wide, decay_wide):
    tokens, inner = cum_wide.shape
    cum_parts = split3(cum_cols[...])
    dt_parts = split3(dt_cols[...])

    def each(index, carry):
        here = chunk_of(index)
        rows = head_rows(index)
        wide = dot(cum_parts[0], rows) + (dot(cum_parts[1], rows) + dot(cum_parts[2], rows))
        cum_wide[:, here] = wide
        dt_wide[:, here] = dot(dt_parts[0], rows) + (
            dot(dt_parts[1], rows) + dot(dt_parts[2], rows)
        )
        decay_wide[:, here] = jnp.broadcast_to(jnp.exp2(wide[tokens - 1 : tokens]), (8, LANES))
        return carry

    lax.fori_loop(0, inner // LANES, each, 0)


def filter_chunk(here, raw, halo, taps, bias, window, act, slope):
    tokens = raw.shape[0]
    window[0:8, :] = halo[:, here].astype(F32)[8:]
    window[8 : 8 + tokens, :] = raw[:, here].astype(F32)
    count = taps.shape[0]
    filtered = bias[:, here] + taps[0:1, here] * window[9 - count : 9 - count + tokens, :]
    for k in range(1, count):
        filtered = filtered + taps[k : k + 1, here] * window[9 - count + k : 9 - count + k + tokens, :]
    gate = sigmoid(filtered)
    result = filtered * gate
    act[:, here] = result
    slope[:, here] = gate + result * (1.0 - gate)
    return result


def in_messages(total, after, each, carry):
    def several(message, carry):
        for j in range(GROUP):
            carry = each(message * GROUP + j, carry)
        after(message)
        return carry

    return lax.fori_loop(0, total // GROUP, several, carry)


def state_phase(
    raw, halo, taps, bias, window, act, slope, cum_wide, dt_wide, key_t, query_t, states, after
):
    tokens, inner = cum_wide.shape
    first = inner // LANES
    key = filter_chunk(pl.ds(inner, LANES), raw, halo, taps, bias, window, act, slope)
    query = filter_chunk(pl.ds(inner + LANES, LANES), raw, halo, taps, bias, window, act, slope)
    high, low = split2(key.T)
    key_t[0], key_t[1] = high, low
    high, low = split2(query.T)
    query_t[0], query_t[1] = high, low

    def each(index, carry):
        here = chunk_of(index)
        values = filter_chunk(here, raw, halo, taps, bias, window, act, slope)
        cum = cum_wide[:, here]
        moved = values * dt_wide[:, here] * jnp.exp2(cum[tokens - 1 : tokens] - cum)
        states[index] = dot3((key_t[0], key_t[1]), split2(moved))
        return carry

    in_messages(first, after, each, 0)


def score_blocks(act, inner, scores):
    half = act.shape[0] // 2
    key = split2(act[:, inner : inner + LANES])
    query = split2(act[:, inner + LANES : inner + 2 * LANES])
    shape = (half, half)
    causal = iota(shape, 0) >= iota(shape, 1)
    for slot, (rows, columns) in enumerate(((0, 0), (1, 1), (1, 0))):
        left = tuple(part[rows * half : (rows + 1) * half] for part in query)
        right = tuple(part[columns * half : (columns + 1) * half] for part in key)
        block = dot3(left, right, NT)
        if rows == columns:
            block = jnp.where(causal, block, 0.0)
        scores[slot] = block


def decay_blocks(index, cum, cum_rows, half, block):
    rows = slice(block * half, (block + 1) * half)
    found = []
    for j in range(2):
        column = jnp.broadcast_to(cum[rows, j * HEAD_DIM : j * HEAD_DIM + 1], (half, half))
        row = cum_rows[2 * index + j][:, rows]
        found.append(jnp.exp2(jnp.minimum(column - row, 0.0)))
    return jnp.concatenate(found, axis=1)


def stacked(block):
    low = low_half(block.shape)
    zero = jnp.zeros_like(block)
    return jnp.concatenate([jnp.where(low, block, zero), jnp.where(low, zero, block)], axis=0)


def inside_phase(act, cum_wide, dt_wide, cum_rows, scores, inside, after):
    tokens, inner = cum_wide.shape
    half = tokens // 2

    def each(index, carry):
        here = chunk_of(index)
        scaled = act[:, here] * dt_wide[:, here]
        cum = cum_wide[:, here]
        for block in range(2):
            rows = slice(block * half, (block + 1) * half)
            weights = decay_blocks(index, cum, cum_rows, half, block)
            score = scores[block]
            weights = jnp.concatenate([score, score], axis=1) * weights
            right = stacked(scaled[rows])
            result = dot3(split2(weights), split2(right))
            if block == 1:
                middle = cum[half - 1 : half]
                moved = scaled[:half] * jnp.exp2(middle - cum[:half])
                result = result + jnp.exp2(cum[half:] - middle) * dot3(
                    split2(scores[2]), split2(moved)
                )
            inside[rows, here] = result
        return carry

    in_messages(inner // LANES, after, each, 0)


def norm_phase(act, cum_wide, inside, entering, skip_wide, gate, norm_weight, gated, scale, low):
    tokens, inner = cum_wide.shape
    query = split2(act[:, inner + LANES : inner + 2 * LANES])

    def each(index, total):
        here = chunk_of(index)
        crossed = jnp.exp2(cum_wide[:, here]) * dot3(query, split2(entering[index]))
        scanned = inside[:, here] + crossed
        inside[:, here] = scanned
        scanned = scanned + skip_wide[:, here] * act[:, here]
        branch = gate[:, here].astype(F32)
        result = scanned * (branch * sigmoid(branch))
        gated[:, here] = result
        return total + result * result

    total = lax.fori_loop(0, inner // LANES, each, jnp.zeros((tokens, LANES), F32))
    mean = jnp.sum(total, axis=1, keepdims=True) / inner
    inverse = lax.rsqrt(mean + EPSILON)
    scale[...] = jnp.broadcast_to(inverse, scale.shape)

    per = low.shape[2] // LANES

    def rounded(index, carry):
        here = chunk_of(index)
        place = pl.ds(pl.multiple_of(index % per * LANES, LANES), LANES)
        result = gated[:, here] * scale[...] * norm_weight[:, here]
        low[index // per, :, place] = result.astype(BF16)
        return carry

    lax.fori_loop(0, inner // LANES, rounded, 0)


def gate_phase(
    act, cum_wide, inside, skip_wide, gate, norm_weight, gated, scale, query_t, cotangent, weight,
    normed_grad, scanned_grad, gate_grad, norm_grad, skip_sum, entering_grad,
    after,
):
    tokens, inner = cum_wide.shape
    own = cotangent[...]

    def first(index, total):
        here = chunk_of(index)
        rows = weight[pl.ds(pl.multiple_of(index * LANES, LANES), LANES), :]
        found = dot(own, rows, NT)
        normed_grad[:, here] = found
        return total + found * norm_weight[:, here] * gated[:, here]

    total = lax.fori_loop(0, inner // LANES, first, jnp.zeros((tokens, LANES), F32))
    inverse = scale[...]
    pull = jnp.sum(total, axis=1, keepdims=True) / inner * inverse * inverse * inverse

    def second(index, carry):
        here = chunk_of(index)
        found = normed_grad[:, here]
        product = gated[:, here]
        norm_grad[:, here] = jnp.broadcast_to(
            jnp.sum(found * product * inverse, axis=0, keepdims=True), (8, LANES)
        )
        down = inverse * (found * norm_weight[:, here]) - product * pull
        branch = gate[:, here].astype(F32)
        opened = sigmoid(branch)
        passed = branch * opened
        values = act[:, here]
        scanned = inside[:, here] + skip_wide[:, here] * values
        gate_grad[:, here] = (down * scanned * (opened + passed * (1.0 - opened))).astype(BF16)
        back = down * passed
        scanned_grad[:, here] = back
        skip_sum[:, here] = jnp.broadcast_to(
            jnp.sum(back * values, axis=0, keepdims=True), (8, LANES)
        )
        moved = back * jnp.exp2(cum_wide[:, here])
        entering_grad[index] = dot3((query_t[0], query_t[1]), split2(moved))
        return carry

    in_messages(inner // LANES, after, second, 0)


def inside_grad_phase(
    act, cum_wide, dt_wide, cum_rows, scores, inside, scanned_grad, entering,
    scaled_grad, score_grad, query_grad, row_sums, after,
):
    tokens, inner = cum_wide.shape
    half = tokens // 2
    score_grad[...] = jnp.zeros_like(score_grad)
    query_grad[...] = jnp.zeros_like(query_grad)
    row_sums[...] = jnp.zeros_like(row_sums)

    def each(index, carry):
        here = chunk_of(index)
        scaled = act[:, here] * dt_wide[:, here]
        cum = cum_wide[:, here]
        back = scanned_grad[:, here]
        middle = cum[half - 1 : half]
        for block in range(2):
            rows = slice(block * half, (block + 1) * half)
            decay = decay_blocks(index, cum, cum_rows, half, block)
            score = scores[block]
            weights = split2(jnp.concatenate([score, score], axis=1) * decay)
            down = split2(back[rows])
            products = dot3(down, split2(stacked(scaled[rows])), NT) * decay
            score_grad[block] += products[:, :half] + products[:, half:]
            found = dot3(weights, down, TN)
            found = jnp.where(low_half((half, LANES)), found[:half], found[half:])
            if block == 0:
                pulled = split2(back[half:] * jnp.exp2(cum[half:] - middle))
                factor = jnp.exp2(middle - cum[:half])
                score_grad[2] += dot3(pulled, split2(scaled[:half] * factor), NT)
                found = found + factor * dot3(split2(scores[2]), pulled, TN)
            scaled_grad[rows, here] = found
        query_grad[...] += dot3(split2(back * jnp.exp2(cum)), split2(entering[index]), NT)
        rows = head_rows(index)
        high, low = split2(back * inside[:, here])
        row_sums[...] += dot(high, rows, NT) + dot(low, rows, NT)
        return carry

    in_messages(inner // LANES, after, each, 0)


def end_phase(
    act, slope, cum_wide, dt_wide, cum_cols, dt_cols, decay_wide, skip_wide, scanned_grad,
    scaled_grad, score_grad, query_grad, row_sums, entering, end_grad, key_grad, skip_sum,
    step, step_bias, decay_row, raw, halo, taps, window, filtered_grad,
    step_grad, filter_sums, head_sums,
):
    tokens, inner = cum_wide.shape
    half = tokens // 2
    key = split2(act[:, inner : inner + LANES])
    query = split2(act[:, inner + LANES : inner + 2 * LANES])
    count = taps.shape[0]

    def finish(here, found):
        pulled = found * slope[:, here]
        filtered_grad[:, here] = pulled
        window[0:8, :] = halo[:, here].astype(F32)[8:]
        window[8 : 8 + tokens, :] = raw[:, here].astype(F32)
        sums = [
            jnp.sum(pulled * window[9 - count + k : 9 - count + k + tokens, :], axis=0, keepdims=True)
            for k in range(count)
        ]
        sums.append(jnp.sum(pulled, axis=0, keepdims=True))
        sums.append(jnp.zeros((8 - len(sums), LANES), F32))
        filter_sums[:, here] = jnp.concatenate(sums, axis=0)

    key_grad[...] = jnp.zeros_like(key_grad)
    zeros = (jnp.zeros((tokens, LANES), F32), jnp.zeros((8, LANES), F32), jnp.zeros((8, LANES), F32))

    def each(index, sums):
        value_sums, last_sums, skip_sums = sums
        here = chunk_of(index)
        values = act[:, here]
        sizes = dt_wide[:, here]
        cum = cum_wide[:, here]
        to_end = jnp.exp2(cum[tokens - 1 : tokens] - cum)
        after = end_grad[index]
        parts = split2(after)
        moved = values * sizes * to_end
        moved_grad = dot3(key, parts)
        key_grad[...] += dot3(split2(moved), parts, NT)
        last = jnp.sum(moved * moved_grad, axis=0, keepdims=True) + decay_wide[0:1, here] * jnp.sum(
            after * entering[index], axis=0, keepdims=True
        )
        scaled = scaled_grad[:, here] + to_end * moved_grad
        rows = head_rows(index)
        high, low = split2(scaled * values)
        value_sums = value_sums + (dot(high, rows, NT) + dot(low, rows, NT))
        parts = split3(jnp.broadcast_to(last, (8, LANES)))
        last_sums = last_sums + (dot(parts[0], rows, NT) + (dot(parts[1], rows, NT) + dot(parts[2], rows, NT)))
        parts = split3(skip_sum[:, here])
        skip_sums = skip_sums + (dot(parts[0], rows, NT) + (dot(parts[1], rows, NT) + dot(parts[2], rows, NT)))
        finish(here, scaled * sizes + skip_wide[:, here] * scanned_grad[:, here])
        return value_sums, last_sums, skip_sums

    value_sums, last_sums, skip_sums = lax.fori_loop(0, inner // LANES, each, zeros)

    shape = (half, half)
    causal = iota(shape, 0) >= iota(shape, 1)
    blocks = [split2(jnp.where(causal, score_grad[slot], 0.0)) for slot in range(2)]
    blocks.append(split2(score_grad[2]))
    first = lambda parts: tuple(part[:half] for part in parts)
    second = lambda parts: tuple(part[half:] for part in parts)
    upper = dot3(blocks[0], first(key))
    lower = dot3(blocks[1], second(key)) + dot3(blocks[2], first(key))
    finish(pl.ds(inner + LANES, LANES), query_grad[...] + jnp.concatenate([upper, lower], axis=0))
    upper = dot3(blocks[0], first(query), TN) + dot3(blocks[2], second(query), TN)
    lower = dot3(blocks[1], second(query), TN)
    finish(pl.ds(inner, LANES), key_grad[...] + jnp.concatenate([upper, lower], axis=0))

    sizes = dt_cols[...]
    cum_grad = row_sums[...] - sizes * value_sums
    at_end = iota((tokens, LANES), 0) == tokens - 1
    cum_grad = cum_grad + jnp.where(at_end, jnp.broadcast_to(last_sums[0:1], (tokens, LANES)), 0.0)
    shape = (tokens, tokens)
    after = jnp.where(iota(shape, 0) <= iota(shape, 1), 1.0, 0.0).astype(BF16)
    parts = split3(cum_grad)
    rate_grad = dot(after, parts[0]) + (dot(after, parts[1]) + dot(after, parts[2]))
    rate = -jnp.exp(decay_row[...])
    heads = step.shape[0]
    shifted = transposed(step[...] + step_bias[...])
    pulled = (value_sums + rate_grad * rate) * sigmoid(shifted)
    pulled = jnp.where(iota((tokens, LANES), 1) < heads, pulled, 0.0)
    step_grad[...] = pulled.T[:heads]
    head_sums[...] = jnp.concatenate(
        [
            jnp.sum(pulled, axis=0, keepdims=True),
            jnp.sum(rate_grad * rate * sizes, axis=0, keepdims=True),
            skip_sums[0:1],
            jnp.zeros((5, LANES), F32),
        ],
        axis=0,
    )


def filter_grad_phase(filtered_grad, following, taps, window, input_grad):
    tokens, channels = filtered_grad.shape
    count = taps.shape[0]

    def each(index, carry):
        here = chunk_of(index)
        window[0:tokens, :] = filtered_grad[:, here]
        window[tokens : tokens + 8, :] = following[:, here]
        total = taps[count - 1 : count, here] * window[0:tokens, :]
        for k in range(count - 1):
            offset = count - 1 - k
            total = total + taps[k : k + 1, here] * window[offset : offset + tokens, :]
        input_grad[:, here] = total.astype(BF16)
        return carry

    lax.fori_loop(0, channels // LANES, each, 0)


def toggled(index, bit):
    return index + bit - 2 * bit * (index // bit % 2)


def weight_phase(columns, cotangents, total):
    peers, tokens, rows = columns.shape

    def each(index, carry):
        here = chunk_of(index)
        found = dot(columns[0, :, here], cotangents[0], TN)
        for peer in range(1, peers):
            found = found + dot(columns[peer, :, here], cotangents[peer], TN)
        total[pl.ds(pl.multiple_of(index * LANES, LANES), LANES), :] = found
        return carry

    lax.fori_loop(0, rows // LANES, each, 0)


def layer_kernel(
    spans, groups,
    raw, gate, step, taps, bias, step_bias, decay_log, decay_row, skip_wide, norm_weight,
    weight, cotangent,
    input_grad, gate_grad, step_grad, weight_grad, small,
    halo, weights, cotangents, act, slope, cum_wide, dt_wide, decay_wide, other_decay,
    cum_rows, cum_cols, dt_cols, key_t, query_t, window, scores,
    states, states_other, entering, inside, gated, scale, low, columns,
    normed_grad, scanned_grad, norm_grad, skip_sum,
    back_states, back_other, end_grad, score_grad, query_grad, row_sums, key_grad,
    filter_sums, head_sums, following, heads_out,
    weight_out, weight_in, weight_all, small_in,
    local_sem, halo_sem, decay_sem, gather_sem, column_sem, ahead_sem, back_sem, next_sem,
    share_sem, small_sem,
):
    q, d = lax.axis_index("seq"), lax.axis_index("dp")
    tokens, channels = raw.shape
    inner = gate.shape[1]
    own_rows = weight.shape[0]
    count = taps.shape[0]
    filtered_grad = act
    scaled_grad = normed_grad

    def remote(source, target, sems, slot, seq=None, dp=None):
        return pltpu.make_async_remote_copy(
            src_ref=source,
            dst_ref=target,
            send_sem=sems.at[0, slot],
            recv_sem=sems.at[1, slot],
            device_id=(q if seq is None else seq, d if dp is None else dp),
            device_id_type=MESH,
        )

    first, last = q == 0, q == spans - 1
    partner = toggled(q, 1)
    odd = q % 2 == 1
    group, groups_along = q // 2, spans // 2

    own_slot = pl.ds(pl.multiple_of(d * own_rows, LANES), own_rows)
    load_weight = pltpu.make_async_copy(weight, weights.at[own_slot], local_sem.at[0])
    load_cotangent = pltpu.make_async_copy(cotangent, cotangents.at[d], local_sem.at[1])
    load_weight.start()
    load_cotangent.start()

    halo_copy = remote(raw.at[tokens - 16 : tokens], halo, halo_sem, 0, seq=q + 1)
    pl.when(jnp.logical_not(last))(halo_copy.start)

    @pl.when(first)
    def _():
        halo[...] = jnp.zeros_like(halo)

    across, beside = toggled(d, 2), toggled(d, 1)

    def slot_of(owner):
        return weights.at[pl.ds(pl.multiple_of(owner * own_rows, LANES), own_rows)]

    def gather(kind, owner, slot, target):
        place = slot_of(owner) if kind == 0 else cotangents.at[owner]
        return remote(place, place, gather_sem, 3 * kind + slot, dp=target)

    load_weight.wait()
    load_cotangent.wait()
    for kind in range(2):
        gather(kind, d, 0, across).start()
        gather(kind, d, 1, beside).start()

    step_phase(step, step_bias, decay_log, cum_rows, cum_cols, dt_cols)
    expand_phase(cum_cols, dt_cols, cum_wide, dt_wide, decay_wide)
    decay_copy = remote(decay_wide, other_decay, decay_sem, 0, seq=partner)
    decay_copy.start()
    pl.when(jnp.logical_not(first))(halo_copy.wait_recv)

    def message(index):
        return pl.ds(index * GROUP, GROUP)

    def pair_copy(source, target, sems, index):
        return remote(source.at[message(index)], target.at[message(index)], sems, index, seq=partner)

    state_phase(
        raw, halo, taps, bias, window, act, slope, cum_wide, dt_wide, key_t, query_t, states,
        lambda index: pair_copy(states, states_other, ahead_sem, index).start(),
    )
    decay_copy.wait()
    score_blocks(act, inner, scores)

    def chain_step(index, own, other, arrived, pair_sem, chain_sem, late, begins, ends, towards):
        pair = pair_copy(own, other, pair_sem, index)
        chain = remote(own.at[message(index)], arrived.at[message(index)], chain_sem, index, seq=towards)
        pair.wait()
        pl.when(jnp.logical_not(begins))(chain.wait_recv)
        for j in range(GROUP):
            at = index * GROUP + j
            here = chunk_of(at)
            mine, theirs = own[at], other[at]
            mine_decay = decay_wide[0:1, here]
            their_decay = other_decay[0:1, here]
            running = jnp.where(begins, 0.0, arrived[at])
            both = jnp.where(late, mine_decay * theirs + mine, their_decay * mine + theirs)
            own[at] = mine_decay * their_decay * running + both
            arrived[at] = jnp.where(late, theirs + their_decay * running, running)
        pl.when(jnp.logical_not(ends))(chain.start)

    def chain_end(index, own, arrived, chain_sem, ends, towards):
        chain = remote(own.at[message(index)], arrived.at[message(index)], chain_sem, index, seq=towards)
        pl.when(jnp.logical_not(ends))(chain.wait_send)

    messages = states.shape[0] // GROUP
    begins, ends = group == 0, group == groups_along - 1

    inside_phase(
        act, cum_wide, dt_wide, cum_rows, scores, inside,
        lambda index: chain_step(
            index, states, states_other, entering, ahead_sem, next_sem.at[0], odd, begins, ends, q + 2
        ),
    )

    gather(0, across, 0, across).wait_recv()
    gather(0, across, 2, beside).start()
    norm_phase(act, cum_wide, inside, entering, skip_wide, gate, norm_weight, gated, scale, low)

    def column_copy(slot, peer):
        return remote(low.at[peer], columns.at[d], column_sem, slot, dp=peer)

    def column_arrival(slot, peer):
        return remote(low.at[peer], columns.at[peer], column_sem, slot, dp=peer)

    peers = (across, toggled(across, 1), beside)
    for slot, peer in enumerate(peers):
        column_copy(slot, peer).start()
    columns[d] = low[d]
    gather(1, across, 0, across).wait_recv()
    gather(1, across, 2, beside).start()
    gather(0, beside, 1, beside).wait_recv()
    gather(0, toggled(across, 1), 2, beside).wait_recv()

    gate_phase(
        act, cum_wide, inside, skip_wide, gate, norm_weight, gated, scale, query_t,
        cotangents.at[d], weights, normed_grad, scanned_grad, gate_grad, norm_grad, skip_sum,
        back_states,
        lambda index: pair_copy(back_states, back_other, back_sem, index).start(),
    )

    bits = []
    while 2 ** len(bits) < spans:
        bits.append(2 ** len(bits))
    size = own_rows
    base = 0
    plan = []
    offset = 0
    for bit in bits:
        mine = q // bit % 2
        if size // 2 % 16 == 0:
            size = size // 2
            keep, give = base + mine * size, base + (1 - mine) * size
            plan.append((bit, True, size, keep, give, offset, mine))
            base = keep
        else:
            plan.append((bit, False, size, base, base, offset, mine))
        offset = offset + size

    def rows_at(start, length):
        return pl.ds(pl.multiple_of(start, 16), length)

    def share_copy(number):
        bit, _, length, _, _, place, _ = plan[number]
        return remote(
            weight_out.at[place : place + length], weight_in.at[place : place + length],
            share_sem, number, seq=toggled(q, bit),
        )

    def share_start(number):
        _, _, length, _, give, place, _ = plan[number]
        weight_out[place : place + length] = weight_grad[rows_at(give, length)].astype(BF16)
        share_copy(number).start()

    def share_finish(number):
        _, halves, length, keep, _, place, _ = plan[number]
        share_copy(number).wait()
        found = weight_in[place : place + length].astype(F32)
        kept = weight_grad[rows_at(keep, length)]
        if not halves:
            kept = weight_out[place : place + length].astype(F32)
        weight_grad[rows_at(keep, length)] = kept + found

    def weights_ready():
        for slot, peer in enumerate(peers):
            column_arrival(slot, peer).wait_recv()
        gather(1, beside, 1, beside).wait_recv()
        gather(1, toggled(across, 1), 2, beside).wait_recv()
        weight_phase(columns, cotangents, weight_grad)
        share_start(0)

    def back_step(index):
        chain_step(
            index, back_states, back_other, end_grad, back_sem, next_sem.at[1],
            jnp.logical_not(odd), ends, begins, q - 2,
        )
        pl.when(index == messages // 2)(weights_ready)

    inside_grad_phase(
        act, cum_wide, dt_wide, cum_rows, scores, inside, scanned_grad, entering,
        scaled_grad, score_grad, query_grad, row_sums, back_step,
    )
    share_finish(0)
    if len(plan) > 1:
        share_start(1)
    end_phase(
        act, slope, cum_wide, dt_wide, cum_cols, dt_cols, decay_wide, skip_wide, scanned_grad,
        scaled_grad, score_grad, query_grad, row_sums, entering, end_grad, key_grad, skip_sum,
        step, step_bias, decay_row, raw, halo, taps, window, filtered_grad,
        step_grad, filter_sums, head_sums,
    )
    heads_out[...] = filtered_grad[0:8, :]
    back_copy = remote(heads_out, following, halo_sem, 1, seq=q - 1)
    pl.when(jnp.logical_not(first))(back_copy.start)

    @pl.when(last)
    def _():
        following[...] = jnp.zeros_like(following)

    small[...] = filter_sums[...]
    small[count + 1 : count + 2, 0:inner] = norm_grad[0:1, :]
    for row in range(3):
        small[count + 2 : count + 3, row * LANES : (row + 1) * LANES] = head_sums[row : row + 1, :]

    steps = [("dp", bit) for bit in (1, 2)] + [("seq", bit) for bit in bits]

    def small_copy(number):
        axis, bit = steps[number]
        target = {"seq": toggled(q, bit)} if axis == "seq" else {"dp": toggled(d, bit)}
        return remote(small_in.at[2 * number], small_in.at[2 * number + 1], small_sem, number, **target)

    def small_start(number):
        small_in[2 * number] = small[...]
        small_copy(number).start()

    def small_finish(number):
        small_copy(number).wait()
        small[...] += small_in[2 * number + 1]

    small_start(0)
    for number in range(1, len(plan)):
        share_finish(number)
        if number + 1 < len(plan):
            share_start(number + 1)
        small_finish(number - 1)
        small_start(number)

    final = plan[-1]
    weight_all[rows_at(base, size)] = weight_grad[rows_at(base, size)].astype(BF16)

    halvings = [number for number in range(len(plan)) if plan[number][1]]

    def spread_copy(number):
        bit, _, length, keep, _, _, _ = plan[number]
        place = weight_all.at[rows_at(keep, length)]
        return remote(place, place, share_sem, len(plan) + number, seq=toggled(q, bit))

    def spread_arrival(number):
        bit, _, length, _, give, _, _ = plan[number]
        place = weight_all.at[rows_at(give, length)]
        return remote(place, place, share_sem, len(plan) + number, seq=toggled(q, bit))

    spread_copy(halvings[-1]).start()
    pl.when(jnp.logical_not(last))(back_copy.wait_recv)
    filter_grad_phase(filtered_grad, following, taps, window, input_grad)
    for number in reversed(halvings):
        spread_arrival(number).wait_recv()
        if number > 0:
            spread_copy(number - 1).start()
    done = len(plan) - 1
    small_finish(done)
    for number in range(done + 1, len(steps)):
        small_start(number)
        small_finish(number)

    def widen(index, carry):
        rows = pl.ds(pl.multiple_of(index * 64, 64), 64)
        weight_grad[rows] = weight_all[rows].astype(F32)
        return carry

    lax.fori_loop(0, own_rows // 64, widen, 0)

    for number in halvings:
        spread_copy(number).wait_send()
    for kind in range(2):
        gather(kind, d, 0, across).wait_send()
        gather(kind, d, 1, beside).wait_send()
        gather(kind, across, 2, beside).wait_send()
    for slot, peer in enumerate(peers):
        column_copy(slot, peer).wait_send()
    pl.when(jnp.logical_not(last))(halo_copy.wait_send)
    pl.when(jnp.logical_not(first))(back_copy.wait_send)
    for index in range(messages):
        chain_end(index, states, entering, next_sem.at[0], ends, q + 2)
        chain_end(index, back_states, end_grad, next_sem.at[1], begins, q - 2)


def body(
    conv_input,
    gate_input,
    step_input,
    filter_taps,
    filter_bias,
    step_bias,
    decay_log,
    skip_gain,
    norm_weight,
    output_weight,
    output_grad,
):
    raw, gate, step, cotangent = conv_input[0], gate_input[0], step_input[0], output_grad[0]
    tokens, channels = raw.shape
    inner = gate.shape[1]
    heads = step.shape[0]
    own_rows, width = output_weight.shape
    count = filter_taps.shape[0]
    spans, groups = lax.axis_size("seq"), lax.axis_size("dp")
    half = tokens // 2
    chunks = inner // LANES
    messages = chunks // GROUP
    assert groups == 4 and tokens % 256 == 0 and inner % (GROUP * LANES) == 0
    levels = spans.bit_length() - 1
    shared, size = 0, own_rows
    for _ in range(levels):
        size = size // 2 if size // 2 % 16 == 0 else size
        shared += size
    wide = pltpu.VMEM((tokens, inner), F32)
    full = pltpu.VMEM((tokens, channels), F32)
    columns = pltpu.VMEM((tokens, LANES), F32)
    row8 = pltpu.VMEM((8, inner), F32)
    stored = pltpu.VMEM((chunks, LANES, LANES), F32)
    turned = pltpu.VMEM((2, LANES, tokens), BF16)
    squares = pltpu.VMEM((3, half, half), F32)
    edge = pltpu.VMEM((8, channels), F32)
    sems = pltpu.SemaphoreType.DMA
    scratch = [
        pltpu.VMEM((16, channels), BF16),
        pltpu.VMEM((groups * own_rows, width), BF16),
        pltpu.VMEM((groups, tokens, width), BF16),
        full, full, wide, wide, row8, row8,
        pltpu.VMEM((heads, 1, tokens), F32), columns, columns, turned, turned,
        pltpu.VMEM((tokens + 8, LANES), F32), squares,
        stored, stored, stored, wide, wide, columns,
        pltpu.VMEM((groups, tokens, own_rows), BF16),
        pltpu.VMEM((groups, tokens, own_rows), BF16),
        wide, wide, row8, row8,
        stored, stored, stored, squares, columns, columns, columns,
        edge, pltpu.VMEM((8, LANES), F32), edge, edge,
        pltpu.VMEM((shared, width), BF16),
        pltpu.VMEM((shared, width), BF16),
        pltpu.VMEM((own_rows, width), BF16),
        pltpu.VMEM((2 * (levels + 2), 8, channels), F32),
        sems((2,)), sems((2, 2)), sems((2, 1)), sems((2, 6)), sems((2, 3)),
        sems((2, messages)), sems((2, messages)), sems((2, 2, messages)),
        sems((2, 2 * levels)), sems((2, levels + 2)),
    ]
    outs = [
        ((tokens, channels), BF16), ((tokens, inner), BF16), ((heads, tokens), F32),
        ((own_rows, width), F32), ((8, channels), F32),
    ]
    args = (
        raw, gate, step, filter_taps, filter_bias[None], step_bias[:, None], decay_log[:, None],
        jnp.pad(decay_log, (0, LANES - heads))[None], jnp.repeat(skip_gain, HEAD_DIM)[None],
        norm_weight[None], output_weight, cotangent,
    )
    vmem = pl.BlockSpec(memory_space=pltpu.VMEM)
    anywhere = pl.BlockSpec(memory_space=pl.ANY)
    input_grad, gate_grad, step_grad, weight_grad, small = pl.pallas_call(
        functools.partial(layer_kernel, spans, groups),
        out_shape=[jax.ShapeDtypeStruct(shape, kind) for shape, kind in outs],
        in_specs=[vmem] * (len(args) - 2) + [anywhere] * 2,
        out_specs=[vmem] * len(outs),
        scratch_shapes=scratch,
        compiler_params=pltpu.CompilerParams(
            vmem_limit_bytes=67043328, has_side_effects=True
        ),
    )(*args)
    head_grads = small[count + 2, : 3 * LANES].reshape(3, LANES)[:, :heads]
    return (
        input_grad[None], gate_grad[None], step_grad[None], weight_grad,
        small[: count + 1], small[count + 1, :inner], head_grads,
    )


def solution(mesh):
    return jax.shard_map(
        body,
        mesh=mesh,
        in_specs=(
            P("dp", "seq", None),
            P("dp", "seq", None),
            P("dp", None, "seq"),
            P(),
            P(),
            P(),
            P(),
            P(),
            P(),
            P("dp", None),
            P("dp", "seq", None),
        ),
        out_specs=(
            P("dp", "seq", None),
            P("dp", "seq", None),
            P("dp", None, "seq"),
            P("dp", None),
            P(),
            P(),
            P(),
        ),
        check_vma=False,
    )
```

time: 418 us -> 211 us (0.50); the launches traced: 411 us -> 210 us
  Pallas kernels: 0 us -> 192 us
  waiting for transfers between devices: 120 us -> 0 us
  other arithmetic: 69.1 us -> 0 us
  matrix products: 64.5 us -> 0 us
  starting transfers between devices: 47.2 us -> 0 us
  blocking collectives: 40 us -> 0 us
  local copies, waits for them, and re-layouts: 54.6 us -> 17.5 us
  between operations: 15.1 us -> 0.66 us
    pallas_call x0 -> x1, Pallas kernels: none -> 192 us  [body(): pl.pallas_call(functools.partial(layer_kernel, spans, groups), out_shape=...]
    all_to_all x9 -> x0, waiting for transfers between devices: 116 us -> none  [the longest x2 48.4 us: carried(): lax.all_to_all(pieces, axis, split_axis=0, concat_axis=0, tiled=True)]
    dot_general x14 -> x0, matrix products: 64.5 us -> none  [the longest x3 30.7 us: finish(): inside = jnp.einsum('hcts,cshp->cthp', weights, scaled, precision=PRECISE)]
    all_to_all x9 -> x0, starting transfers between devices: 41 us -> none  [the longest x2 10.3 us: carried(): lax.all_to_all(pieces, axis, split_axis=0, concat_axis=0, tiled=True)]
    all_gather x1 -> x0, blocking collectives: 40 us -> none  [summed_everywhere(): total = lax.all_gather(jnp.sum(terms, axis=0), axes, axis=0, tiled=True)]
    reduce_sum x8 -> x0, other arithmetic: 20.2 us -> none  [the longest x1 5.43 us: prepare(): filtered = filtered + filter_taps[offset] * extended[offset:offset + length]]
    mul x9 -> x0, other arithmetic: 14.3 us -> none  [the longest x1 4.23 us: finish(): result = inside + from_state + skip_gain[:, None] * values]
    unnamed x10 -> x0, other arithmetic: 12.2 us -> none
  transfers between devices with their start and end apart: 13 -> 0, of which waited for: 7 -> 0; matrix products, arithmetic and copies ran while one was open for 40% -> 0% of each run, Pallas kernels for 0% -> 0%
where the time goes in v1:
time: 211 us; the launch traced here: 210 us
  Pallas kernels  192 us (91%)
  local copies, waits for them, and re-layouts  17.5 us (8%)
    pallas_call x1, Pallas kernels, body(): pl.pallas_call(functools.partial(layer_kernel, spans, groups), out_shape=...  192 us
    unnamed x13, local copies, waits for them, and re-layouts  6.74 us

profile of v1, /device:TPU:0, one launch (start us, length us, event | category | flops | bytes accessed | tf_op | source)
XLA Modules:
  0.0 210.3 jit_solution(9952530272987487411)
XLA Ops:
  0.6 1.3 broadcast_in_dim.27.bias
  1.9 1.3 copy.18.step_bias
  3.3 1.3 copy.19.decay_log
  4.6 1.2 pad_bitcast_fusion.decay_row
  5.8 0.7 broadcast_in_dim.31
  6.5 0.7 broadcast_in_dim_reshape.3.skip_wide
  7.2 1.3 broadcast_in_dim.32.norm_weight
  8.5 192.1 %shard_map.162 = (bf16[256,2816]{1,0:T(8,128)(2,1)}, bf16[256,2560]{1,0:T(8,128)(2,1)}, f32[40,256]{1,0:T(8,128)}, f32[640,1280]{1,0:T(8,128)}, f32[8,2816]{1,0:T(8,128)}) custom-call(bf16[256,2816]{1,0:T(8,128)(2,1)} %bitcast.15, bf16[256,2560]{1,0:T(8,128)(2,1)} %bitcast.17, f32[40,256]{1,0:T(8,128)} %bitcast.20, f32[4,2816]{1,0:T(4,128)} %taps.1, ...), custom_call_target="tpu_custom_call" | custom-call | tf_op jit(solution)/shard_map/pallas_call | solution.py:832
  200.6 0.0 copy-start.1
  200.6 1.6 slice_reduce_fusion
  202.2 1.3 slice_reduce_fusion.1
  203.5 0.0 copy-start
  203.5 2.7 %copy.25 = bf16[1,256,2816]{2,1,0:T(8,128)(2,1)} copy(bf16[1,256,2816]{2,1,0:T(8,128)(2,1)} %bitcast.14) | data formatting | bytes 2883584
  206.2 0.0 copy-done.1
  206.2 0.0 copy-start.3
  206.2 1.1 copy.26
  207.3 0.0 copy-done.3
  207.3 0.6 copy.27
  207.9 0.0 copy-done
  207.9 0.0 copy-start.2
  207.9 1.7 copy.28
  209.6 0.0 copy-done.2
  209.6 0.6 copy.29
Async XLA Ops:
  200.6 5.6 %copy-start.1 = (bf16[256,2560]{1,0:T(8,128)(2,1)S(1)}, bf16[256,2560]{1,0:T(8,128)(2,1)}, u32[]{:S(2)}) copy-start(bf16[256,2560]{1,0:T(8,128)(2,1)} %get-tuple-element.13) | copy-start | bytes 3932164
  203.5 4.4 %copy-start = (f32[640,1280]{1,0:T(8,128)S(1)}, f32[640,1280]{1,0:T(8,128)}, u32[]{:S(2)}) copy-start(f32[640,1280]{1,0:T(8,128)} %get-tuple-element.27) | copy-start | bytes 9830404
  206.2 1.1 copy-start.3
  207.9 1.7 copy-start.2

commit v2 on v1

v2 whole, which is shorter than its diff:
```python
import functools

import jax
import jax.numpy as jnp
from jax import lax
from jax.experimental import pallas as pl
from jax.experimental.pallas import tpu as pltpu
from jax.sharding import PartitionSpec as P

F32 = jnp.float32
BF16 = jnp.bfloat16
EPSILON = 1e-05
LOG2E = 1.4426950408889634
LANES = 128
HEAD_DIM = 64
MESH = pl.DeviceIdType.MESH
CHAIN_HOOKS = (6, 9)
FAR_HOOKS = (4, 8)
NEAR_HOOKS = (6, 9)
NN = (((1,), (0,)), ((), ()))
NT = (((1,), (1,)), ((), ()))
TN = (((0,), (0,)), ((), ()))


def dot(a, b, dims=NN):
    return lax.dot_general(a, b, dims, preferred_element_type=F32)


def rounded_high(a):
    scaled = a * 65537.0
    return scaled - (scaled - a)


def split2(a):
    high = rounded_high(a)
    return high.astype(BF16), (a - high).astype(BF16)


def split3(a):
    high = rounded_high(a)
    rest = a - high
    middle = rounded_high(rest)
    return high.astype(BF16), middle.astype(BF16), (rest - middle).astype(BF16)


def dot3(a, b, dims=NN):
    return dot(a[0], b[0], dims) + (dot(a[0], b[1], dims) + dot(a[1], b[0], dims))


def chunk_of(index):
    return pl.ds(pl.multiple_of(index * LANES, LANES), LANES)


def iota(shape, dim):
    return lax.broadcasted_iota(jnp.int32, shape, dim)


def low_half(shape):
    return iota(shape, 1) < HEAD_DIM


def head_rows(index):
    shape = (LANES, LANES)
    wanted = 2 * index + jnp.where(low_half(shape), 0, 1)
    return jnp.where(iota(shape, 0) == wanted, 1.0, 0.0).astype(BF16)


def sigmoid(a):
    return 1.0 / (1.0 + jnp.exp(-a))


def transposed(rows):
    heads, tokens = rows.shape
    padded = jnp.concatenate([rows, jnp.zeros((LANES - heads, tokens), F32)], axis=0)
    return padded.T


def padded_row(row):
    short = row[...]
    return jnp.concatenate([short, jnp.zeros((1, LANES - short.shape[1]), F32)], axis=1)


def column_of(row):
    return jnp.broadcast_to(padded_row(row), (LANES, LANES)).T[: row.shape[1], 0:1]


def step_phase(step, step_bias, decay_log, cum_rows, cum_cols, dt_cols):
    shifted = step[...] + column_of(step_bias)
    sizes = jnp.maximum(shifted, 0.0) + jnp.log1p(jnp.exp(-jnp.abs(shifted)))
    rates = -jnp.exp(column_of(decay_log)) * sizes
    tokens = rates.shape[1]
    shape = (tokens, tokens)
    before = jnp.where(iota(shape, 0) <= iota(shape, 1), 1.0, 0.0).astype(BF16)
    high, middle, low = split3(rates)
    cumulative = (dot(high, before) + (dot(middle, before) + dot(low, before))) * LOG2E
    for head in range(rates.shape[0]):
        cum_rows[head] = cumulative[head : head + 1]
    cum_cols[...] = transposed(cumulative)
    dt_cols[...] = transposed(sizes)


def expand_phase(cum_cols, dt_cols, skip_gain, cum_wide, dt_wide, decay_wide, skip_wide):
    tokens, inner = cum_wide.shape
    cum_parts = split3(cum_cols[...])
    dt_parts = split3(dt_cols[...])
    skip_parts = split3(jnp.broadcast_to(padded_row(skip_gain), (8, LANES)))

    def each(index, carry):
        here = chunk_of(index)
        rows = head_rows(index)
        wide = dot(cum_parts[0], rows) + (dot(cum_parts[1], rows) + dot(cum_parts[2], rows))
        cum_wide[:, here] = wide
        skip_wide[:, here] = dot(skip_parts[0], rows) + (
            dot(skip_parts[1], rows) + dot(skip_parts[2], rows)
        )
        dt_wide[:, here] = dot(dt_parts[0], rows) + (
            dot(dt_parts[1], rows) + dot(dt_parts[2], rows)
        )
        decay_wide[:, here] = jnp.broadcast_to(jnp.exp2(wide[tokens - 1 : tokens]), (8, LANES))
        return carry

    lax.fori_loop(0, inner // LANES, each, 0, unroll=4)


def filter_chunk(index, slot, here, raw, halo, taps, bias, windows, act, slope):
    tokens = raw.shape[0]
    window = windows.at[slot]
    window[0:8, :] = halo[:, here].astype(F32)[8:]
    window[8 : 8 + tokens, :] = raw[:, here].astype(F32)
    count = taps.shape[0]
    filtered = bias[pl.ds(index, 1), :] + taps[0:1, here] * window[9 - count : 9 - count + tokens, :]
    for k in range(1, count):
        filtered = filtered + taps[k : k + 1, here] * window[9 - count + k : 9 - count + k + tokens, :]
    gate = sigmoid(filtered)
    result = filtered * gate
    act[:, here] = result
    slope[:, here] = gate + result * (1.0 - gate)
    return result


def in_pairs(total, before, after, each, carry):
    def several(number, carry):
        if before is not None:
            before(number)
        for j in range(2):
            carry = each(2 * number + j, carry, j)
        if after is not None:
            after(number)
        return carry

    return lax.fori_loop(0, total // 2, several, carry)


def state_phase(
    raw, halo, taps, bias, window, act, slope, cum_wide, dt_wide, key_t, query_t, states, after
):
    tokens, inner = cum_wide.shape
    first = inner // LANES
    key = filter_chunk(first, 0, pl.ds(inner, LANES), raw, halo, taps, bias, window, act, slope)
    query = filter_chunk(first + 1, 1, pl.ds(inner + LANES, LANES), raw, halo, taps, bias, window, act, slope)
    high, low = split2(key.T)
    key_t[0], key_t[1] = high, low
    high, low = split2(query.T)
    query_t[0], query_t[1] = high, low

    def each(index, carry, slot):
        here = chunk_of(index)
        values = filter_chunk(index, slot, here, raw, halo, taps, bias, window, act, slope)
        cum = cum_wide[:, here]
        moved = values * dt_wide[:, here] * jnp.exp2(cum[tokens - 1 : tokens] - cum)
        states[index] = dot3((key_t[0], key_t[1]), split2(moved))
        return carry

    in_pairs(first, None, after, each, 0)


def score_blocks(act, inner, scores):
    half = act.shape[0] // 2
    key = split2(act[:, inner : inner + LANES])
    query = split2(act[:, inner + LANES : inner + 2 * LANES])
    shape = (half, half)
    causal = iota(shape, 0) >= iota(shape, 1)
    for slot, (rows, columns) in enumerate(((0, 0), (1, 1), (1, 0))):
        left = tuple(part[rows * half : (rows + 1) * half] for part in query)
        right = tuple(part[columns * half : (columns + 1) * half] for part in key)
        block = dot3(left, right, NT)
        if rows == columns:
            block = jnp.where(causal, block, 0.0)
        scores[slot] = block


def decay_blocks(index, cum, cum_rows, half, block):
    rows = slice(block * half, (block + 1) * half)
    found = []
    for j in range(2):
        column = jnp.broadcast_to(cum[rows, j * HEAD_DIM : j * HEAD_DIM + 1], (half, half))
        row = cum_rows[2 * index + j][:, rows]
        found.append(jnp.exp2(jnp.minimum(column - row, 0.0)))
    return jnp.concatenate(found, axis=1)


def stacked(block):
    low = low_half(block.shape)
    zero = jnp.zeros_like(block)
    return jnp.concatenate([jnp.where(low, block, zero), jnp.where(low, zero, block)], axis=0)


def inside_phase(act, cum_wide, dt_wide, cum_rows, scores, inside, before, after):
    tokens, inner = cum_wide.shape
    half = tokens // 2

    def each(index, carry, slot):
        here = chunk_of(index)
        scaled = act[:, here] * dt_wide[:, here]
        cum = cum_wide[:, here]
        for block in range(2):
            rows = slice(block * half, (block + 1) * half)
            weights = decay_blocks(index, cum, cum_rows, half, block)
            score = scores[block]
            weights = jnp.concatenate([score, score], axis=1) * weights
            right = stacked(scaled[rows])
            result = dot3(split2(weights), split2(right))
            if block == 1:
                middle = cum[half - 1 : half]
                moved = scaled[:half] * jnp.exp2(middle - cum[:half])
                result = result + jnp.exp2(cum[half:] - middle) * dot3(
                    split2(scores[2]), split2(moved)
                )
            inside[rows, here] = result
        return carry

    in_pairs(inner // LANES, before, after, each, 0)


def norm_phase(act, cum_wide, inside, entering, skip_wide, gate, norm_weight, gated, scale, low):
    tokens, inner = cum_wide.shape
    query = split2(act[:, inner + LANES : inner + 2 * LANES])

    def each(index, total):
        here = chunk_of(index)
        crossed = jnp.exp2(cum_wide[:, here]) * dot3(query, split2(entering[index]))
        scanned = inside[:, here] + crossed
        inside[:, here] = scanned
        scanned = scanned + skip_wide[0:1, here] * act[:, here]
        branch = gate[:, here].astype(F32)
        result = scanned * (branch * sigmoid(branch))
        gated[:, here] = result
        return total + result * result

    total = lax.fori_loop(0, inner // LANES, each, jnp.zeros((tokens, LANES), F32), unroll=2)
    mean = jnp.sum(total, axis=1, keepdims=True) / inner
    inverse = lax.rsqrt(mean + EPSILON)
    scale[...] = jnp.broadcast_to(inverse, scale.shape)

    per = low.shape[2] // LANES

    def rounded(index, carry):
        here = chunk_of(index)
        place = pl.ds(pl.multiple_of(index % per * LANES, LANES), LANES)
        result = gated[:, here] * scale[...] * norm_weight[pl.ds(index, 1), :]
        low[index // per, :, place] = result.astype(BF16)
        return carry

    lax.fori_loop(0, inner // LANES, rounded, 0)


def gate_phase(
    act, cum_wide, inside, skip_wide, gate, norm_weight, gated, scale, query_t,
    chip, normed_sent, normed_grad, scanned_grad, gate_grad, norm_grad, skip_sum, entering_grad,
    after,
):
    tokens, inner = cum_wide.shape

    per = normed_grad.shape[2] // LANES

    def normed_at(index):
        return normed_grad[index // per, :, chunk_of(index % per)]

    def first(index, total):
        here = chunk_of(index)
        slot, place = index // per, chunk_of(index % per)
        sent = normed_sent[slot, :, place].astype(F32)
        found = jnp.where(slot // 2 == chip, normed_grad[slot, :, place], sent)
        normed_grad[slot, :, place] = found
        return total + found * norm_weight[pl.ds(index, 1), :] * gated[:, here]

    total = lax.fori_loop(0, inner // LANES, first, jnp.zeros((tokens, LANES), F32), unroll=2)
    inverse = scale[...]
    pull = jnp.sum(total, axis=1, keepdims=True) / inner * inverse * inverse * inverse

    def second(index, carry, slot):
        here = chunk_of(index)
        found = normed_at(index)
        product = gated[:, here]
        norm_grad[:, here] = jnp.broadcast_to(
            jnp.sum(found * product * inverse, axis=0, keepdims=True), (8, LANES)
        )
        down = inverse * (found * norm_weight[pl.ds(index, 1), :]) - product * pull
        branch = gate[:, here].astype(F32)
        opened = sigmoid(branch)
        passed = branch * opened
        values = act[:, here]
        scanned = inside[:, here] + skip_wide[0:1, here] * values
        gate_grad[:, here] = (down * scanned * (opened + passed * (1.0 - opened))).astype(BF16)
        back = down * passed
        scanned_grad[:, here] = back
        skip_sum[:, here] = jnp.broadcast_to(
            jnp.sum(back * values, axis=0, keepdims=True), (8, LANES)
        )
        moved = back * jnp.exp2(cum_wide[:, here])
        entering_grad[index] = dot3((query_t[0], query_t[1]), split2(moved))
        return carry

    in_pairs(inner // LANES, None, after, second, 0)


def inside_grad_phase(
    act, cum_wide, dt_wide, cum_rows, scores, inside, scanned_grad, entering,
    scaled_grad, score_grad, query_grad, row_sums, before, after,
):
    tokens, inner = cum_wide.shape
    half = tokens // 2
    score_grad[...] = jnp.zeros_like(score_grad)
    query_grad[...] = jnp.zeros_like(query_grad)
    row_sums[...] = jnp.zeros_like(row_sums)

    def each(index, carry, slot):
        here = chunk_of(index)
        scaled = act[:, here] * dt_wide[:, here]
        cum = cum_wide[:, here]
        back = scanned_grad[:, here]
        middle = cum[half - 1 : half]
        for block in range(2):
            rows = slice(block * half, (block + 1) * half)
            decay = decay_blocks(index, cum, cum_rows, half, block)
            score = scores[block]
            weights = split2(jnp.concatenate([score, score], axis=1) * decay)
            down = split2(back[rows])
            products = dot3(down, split2(stacked(scaled[rows])), NT) * decay
            score_grad[block] += products[:, :half] + products[:, half:]
            found = dot3(weights, down, TN)
            found = jnp.where(low_half((half, LANES)), found[:half], found[half:])
            if block == 0:
                pulled = split2(back[half:] * jnp.exp2(cum[half:] - middle))
                factor = jnp.exp2(middle - cum[:half])
                score_grad[2] += dot3(pulled, split2(scaled[:half] * factor), NT)
                found = found + factor * dot3(split2(scores[2]), pulled, TN)
            scaled_grad[rows, here] = found
        query_grad[...] += dot3(split2(back * jnp.exp2(cum)), split2(entering[index]), NT)
        rows = head_rows(index)
        high, low = split2(back * inside[:, here])
        row_sums[...] += dot(high, rows, NT) + dot(low, rows, NT)
        return carry

    in_pairs(inner // LANES, before, after, each, 0)


def end_phase(
    act, slope, cum_wide, dt_wide, cum_cols, dt_cols, decay_wide, skip_wide, scanned_grad,
    scaled_grad, score_grad, query_grad, row_sums, entering, end_grad, key_grad, skip_sum,
    step, step_bias, decay_log, raw, halo, taps, windows, filtered_grad,
    step_grad, filter_sums, head_sums, before_pair, after_pair,
):
    tokens, inner = cum_wide.shape
    half = tokens // 2
    key = split2(act[:, inner : inner + LANES])
    query = split2(act[:, inner + LANES : inner + 2 * LANES])
    count = taps.shape[0]

    def finish(slot, here, found):
        pulled = found * slope[:, here]
        filtered_grad[:, here] = pulled
        window = windows.at[slot]
        window[0:8, :] = halo[:, here].astype(F32)[8:]
        window[8 : 8 + tokens, :] = raw[:, here].astype(F32)
        sums = [
            jnp.sum(pulled * window[9 - count + k : 9 - count + k + tokens, :], axis=0, keepdims=True)
            for k in range(count)
        ]
        sums.append(jnp.sum(pulled, axis=0, keepdims=True))
        sums.append(jnp.zeros((8 - len(sums), LANES), F32))
        filter_sums[:, here] = jnp.concatenate(sums, axis=0)

    key_grad[...] = jnp.zeros_like(key_grad)
    zeros = (jnp.zeros((tokens, LANES), F32), jnp.zeros((8, LANES), F32), jnp.zeros((8, LANES), F32))

    def each(index, sums, slot):
        value_sums, last_sums, skip_sums = sums
        here = chunk_of(index)
        values = act[:, here]
        sizes = dt_wide[:, here]
        cum = cum_wide[:, here]
        to_end = jnp.exp2(cum[tokens - 1 : tokens] - cum)
        after = end_grad[index]
        parts = split2(after)
        moved = values * sizes * to_end
        moved_grad = dot3(key, parts)
        key_grad[...] += dot3(split2(moved), parts, NT)
        last = jnp.sum(moved * moved_grad, axis=0, keepdims=True) + decay_wide[0:1, here] * jnp.sum(
            after * entering[index], axis=0, keepdims=True
        )
        scaled = scaled_grad[:, here] + to_end * moved_grad
        rows = head_rows(index)
        high, low = split2(scaled * values)
        value_sums = value_sums + (dot(high, rows, NT) + dot(low, rows, NT))
        parts = split3(jnp.broadcast_to(last, (8, LANES)))
        last_sums = last_sums + (dot(parts[0], rows, NT) + (dot(parts[1], rows, NT) + dot(parts[2], rows, NT)))
        parts = split3(skip_sum[:, here])
        skip_sums = skip_sums + (dot(parts[0], rows, NT) + (dot(parts[1], rows, NT) + dot(parts[2], rows, NT)))
        finish(slot, here, scaled * sizes + skip_wide[0:1, here] * scanned_grad[:, here])
        return value_sums, last_sums, skip_sums

    value_sums, last_sums, skip_sums = in_pairs(inner // LANES, before_pair, after_pair, each, zeros)

    shape = (half, half)
    causal = iota(shape, 0) >= iota(shape, 1)
    blocks = [split2(jnp.where(causal, score_grad[slot], 0.0)) for slot in range(2)]
    blocks.append(split2(score_grad[2]))
    first = lambda parts: tuple(part[:half] for part in parts)
    second = lambda parts: tuple(part[half:] for part in parts)
    upper = dot3(blocks[0], first(key))
    lower = dot3(blocks[1], second(key)) + dot3(blocks[2], first(key))
    finish(1, pl.ds(inner + LANES, LANES), query_grad[...] + jnp.concatenate([upper, lower], axis=0))
    upper = dot3(blocks[0], first(query), TN) + dot3(blocks[2], second(query), TN)
    lower = dot3(blocks[1], second(query), TN)
    finish(0, pl.ds(inner, LANES), key_grad[...] + jnp.concatenate([upper, lower], axis=0))

    sizes = dt_cols[...]
    cum_grad = row_sums[...] - sizes * value_sums
    at_end = iota((tokens, LANES), 0) == tokens - 1
    cum_grad = cum_grad + jnp.where(at_end, jnp.broadcast_to(last_sums[0:1], (tokens, LANES)), 0.0)
    shape = (tokens, tokens)
    after = jnp.where(iota(shape, 0) <= iota(shape, 1), 1.0, 0.0).astype(BF16)
    parts = split3(cum_grad)
    rate_grad = dot(after, parts[0]) + (dot(after, parts[1]) + dot(after, parts[2]))
    rate = -jnp.exp(padded_row(decay_log))
    heads = step.shape[0]
    shifted = transposed(step[...] + column_of(step_bias))
    pulled = (value_sums + rate_grad * rate) * sigmoid(shifted)
    pulled = jnp.where(iota((tokens, LANES), 1) < heads, pulled, 0.0)
    step_grad[...] = pulled.T[:heads]
    head_sums[...] = jnp.concatenate(
        [
            jnp.sum(pulled, axis=0, keepdims=True),
            jnp.sum(rate_grad * rate * sizes, axis=0, keepdims=True),
            skip_sums[0:1],
            jnp.zeros((5, LANES), F32),
        ],
        axis=0,
    )


def filter_grad_phase(filtered_grad, following, taps, windows, input_grad):
    tokens, channels = filtered_grad.shape
    count = taps.shape[0]

    def each(index, carry, slot):
        here = chunk_of(index)
        window = windows.at[slot]
        window[0:tokens, :] = filtered_grad[:, here]
        window[tokens : tokens + 8, :] = following[:, here]
        total = taps[count - 1 : count, here] * window[0:tokens, :]
        for k in range(count - 1):
            offset = count - 1 - k
            total = total + taps[k : k + 1, here] * window[offset : offset + tokens, :]
        input_grad[:, here] = total.astype(BF16)
        return carry

    in_pairs(channels // LANES, None, None, each, 0)


def toggled(index, bit):
    return index + bit - 2 * bit * (index // bit % 2)


def weight_phase(columns, cotangents, total):
    peers, tokens, rows = columns.shape

    def each(index, carry):
        here = chunk_of(index)
        found = dot(columns[0, :, here], cotangents[0], TN)
        for peer in range(1, peers):
            found = found + dot(columns[peer, :, here], cotangents[peer], TN)
        total[pl.ds(pl.multiple_of(index * LANES, LANES), LANES), :] = found
        return carry

    lax.fori_loop(0, rows // LANES, each, 0)


def layer_kernel(
    spans, groups,
    raw, step, taps, bias, step_bias, decay_log, skip_gain, norm_weight,
    weight, cotangent, gate_in,
    input_grad, gate_out, step_grad, weight_result, filter_out, norm_out, head_out,
    gate, gate_grad, weight_grad, small, skip_wide, halo, weights, cotangents, act, slope, cum_wide, dt_wide, decay_wide, other_decay,
    cum_rows, cum_cols, dt_cols, key_t, query_t, window, scores,
    states, states_other, entering, inside, gated, scale, low, columns,
    normed_grad, normed_sent, partial_beside, partials, scaled_grad, scanned_grad, norm_grad, skip_sum,
    back_states, back_other, end_grad, score_grad, query_grad, row_sums, key_grad,
    filter_sums, head_sums, following, heads_out,
    weight_out, weight_in, weight_all, small_in,
    local_sem, halo_sem, decay_sem, gather_sem, partial_sem, column_sem, ahead_sem, back_sem, next_sem, return_sem,
    share_sem, small_sem,
):
    q, d = lax.axis_index("seq"), lax.axis_index("dp")
    tokens, channels = raw.shape
    inner = gate_in.shape[1]
    own_rows = weight.shape[0]
    count = taps.shape[0]
    filtered_grad = act

    def remote(source, target, sems, slot, seq=None, dp=None):
        return pltpu.make_async_remote_copy(
            src_ref=source,
            dst_ref=target,
            send_sem=sems.at[0, slot],
            recv_sem=sems.at[1, slot],
            device_id=(q if seq is None else seq, d if dp is None else dp),
            device_id_type=MESH,
        )

    first, last = q == 0, q == spans - 1
    partner = toggled(q, 1)
    odd = q % 2 == 1
    group, groups_along = q // 2, spans // 2

    load_weight = pltpu.make_async_copy(weight, weights, local_sem.at[0])
    load_cotangent = pltpu.make_async_copy(cotangent, cotangents.at[d], local_sem.at[1])
    load_gate = pltpu.make_async_copy(gate_in, gate, local_sem.at[2])
    load_cotangent.start()
    load_weight.start()
    load_gate.start()

    across, beside = toggled(d, 2), toggled(d, 1)
    bits = []
    while 2 ** len(bits) < spans:
        bits.append(2 ** len(bits))
    barrier = pltpu.get_barrier_semaphore()

    def greet(seq, dp):
        pl.semaphore_signal(barrier, inc=1, device_id=(seq, dp), device_id_type=MESH)

    for other in (across, beside, toggled(across, 1)):
        greet(q, other)
    for bit in bits:
        greet(toggled(q, bit), d)
    expected = 3 + len(bits)
    for distance in (1, 2):
        below, above = q >= distance, q < spans - distance
        pl.when(below)(lambda distance=distance: greet(q - distance, d))
        pl.when(above)(lambda distance=distance: greet(q + distance, d))
        expected = expected + jnp.where(below, 1, 0) + jnp.where(above, 1, 0)

    with jax.named_scope("steps"):
        step_phase(step, step_bias, decay_log, cum_rows, cum_cols, dt_cols)
    with jax.named_scope("barrier"):
        pl.semaphore_wait(barrier, expected)

    with jax.named_scope("halo_start"):
        halo_copy = remote(raw.at[tokens - 16 : tokens], halo, halo_sem, 0, seq=q + 1)
    pl.when(jnp.logical_not(last))(halo_copy.start)

    @pl.when(first)
    def _():
        halo[...] = jnp.zeros_like(halo)

    diagonal = toggled(across, 1)

    def gather(owner, slot, target):
        place = cotangents.at[owner]
        return remote(place, place, gather_sem, slot, dp=target)

    load_cotangent.wait()
    gather(d, 0, across).start()
    gather(d, 1, beside).start()

    with jax.named_scope("expand"):
        expand_phase(cum_cols, dt_cols, skip_gain, cum_wide, dt_wide, decay_wide, skip_wide)
    decay_copy = remote(decay_wide, other_decay, decay_sem, 0, seq=partner)
    decay_copy.start()
    pl.when(jnp.logical_not(first))(halo_copy.wait_recv)

    side = q % 2

    def pair_copy(source, target, sems, number, arrival=False):
        at = 2 * number + (side if arrival else 1 - side)
        return remote(source.at[at], target.at[at], sems, number, seq=partner)

    with jax.named_scope("states"):
        state_phase(
            raw, halo, taps, bias, window, act, slope, cum_wide, dt_wide, key_t, query_t, states,
            lambda number: pair_copy(states, states_other, ahead_sem, number).start(),
        )
    with jax.named_scope("decay"):
        decay_copy.wait()
    score_blocks(act, inner, scores)

    def chain_copy(own, arrived, sems, number, towards):
        at = 2 * number + side
        return remote(own.at[at], arrived.at[at], sems, number, seq=towards)

    def return_copy(other, arrived, sems, number, arrival=False):
        at = 2 * number + (1 - side if arrival else side)
        return remote(other.at[at], arrived.at[at], sems, number, seq=partner)

    def chain_step(number, own, other, arrived, sems, late, begins, ends, towards):
        pair_sem, chain_sem, return_sem = sems
        chain = chain_copy(own, arrived, chain_sem, number, towards)
        with jax.named_scope("pair_wait"):
            pair_copy(own, other, pair_sem, number, arrival=True).wait_recv()
        with jax.named_scope("chain_wait"):
            pl.when(jnp.logical_not(begins))(chain.wait_recv)
        at = 2 * number + side
        here = chunk_of(at)
        mine, theirs = own[at], other[at]
        mine_decay, their_decay = decay_wide[0:1, here], other_decay[0:1, here]
        running = jnp.where(begins, 0.0, arrived[at])
        both = jnp.where(late, mine_decay * theirs + mine, their_decay * mine + theirs)
        own[at] = mine_decay * their_decay * running + both
        pl.when(jnp.logical_not(ends))(chain.start)
        arrived[at] = jnp.where(late, theirs + their_decay * running, running)
        other[at] = jnp.where(late, running, mine + mine_decay * running)
        return_copy(other, arrived, return_sem, number).start()

    def chain_end(number, own, other, arrived, sems, ends, towards):
        pair_sem, chain_sem, return_sem = sems
        pair_copy(own, other, pair_sem, number).wait_send()
        chain = chain_copy(own, arrived, chain_sem, number, towards)
        pl.when(jnp.logical_not(ends))(chain.wait_send)
        return_copy(other, arrived, return_sem, number).wait_send()

    messages = states.shape[0] // 2
    ahead_sems = (ahead_sem, next_sem.at[0], return_sem.at[0])
    back_sems = (back_sem, next_sem.at[1], return_sem.at[1])
    begins, ends = group == 0, group == groups_along - 1

    per_slot = own_rows // LANES
    owners = (d, beside, across, diagonal)
    load_weight.wait()

    def partial_copy(slot, arrival=False):
        owner = owners[slot]
        lands = owner if arrival else d
        if slot == 1:
            return remote(partial_beside, normed_grad.at[lands], partial_sem, 0, dp=owner)
        return remote(partials.at[slot - 2], normed_sent.at[lands], partial_sem, slot - 1, dp=owner)

    def partial_chunk(number):
        slot = number // per_slot
        owner = owners[3]
        for other in (2, 1, 0):
            owner = jnp.where(slot == other, owners[other], owner)
        index = number % per_slot
        rows = weights[pl.ds(pl.multiple_of(index * LANES, LANES), LANES), :]
        found = dot(cotangents[owner], rows, NT)

        @pl.when(slot == 0)
        def _():
            normed_grad[d, :, chunk_of(index)] = found

        @pl.when(slot == 1)
        def _():
            partial_beside[:, chunk_of(index)] = found

        @pl.when(slot > 1)
        def _():
            partials[slot - 2, :, chunk_of(index)] = found.astype(BF16)

        for slot in (1, 2, 3):
            pl.when(number == (slot + 1) * per_slot - 1)(partial_copy(slot).start)

    early = group < 2

    def across_arrives():
        gather(across, 0, across).wait_recv()
        gather(across, 2, beside).start()

    def ahead_before(number):
        @pl.when((number == 0) & jnp.logical_not(early))
        def _():
            gather(beside, 1, beside).wait_recv()

            def several(first, last):
                def each(at, carry):
                    partial_chunk(at)
                    return carry

                lax.fori_loop(first * per_slot, last * per_slot, each, 0)

            several(0, 2)
            across_arrives()
            several(2, 3)
            gather(diagonal, 2, beside).wait_recv()
            several(3, 4)

    def ahead_step(number):
        chain_step(
            number, states, states_other, entering, ahead_sems, odd, begins, ends, q + 2
        )

        @pl.when(early)
        def _():
            pl.when(number == per_slot // 2)(gather(beside, 1, beside).wait_recv)
            pl.when(number == per_slot)(across_arrives)
            pl.when(number == per_slot + per_slot // 2)(gather(diagonal, 2, beside).wait_recv)
            for j in range(2):
                partial_chunk(2 * number + j)

    with jax.named_scope("inside"):
        inside_phase(
            act, cum_wide, dt_wide, cum_rows, scores, inside, ahead_before, ahead_step,
        )

    with jax.named_scope("return_wait"):
        for number in range(messages):
            return_copy(states_other, entering, ahead_sems[2], number, arrival=True).wait_recv()
    load_gate.wait()
    with jax.named_scope("norm"):
        norm_phase(act, cum_wide, inside, entering, skip_wide, gate, norm_weight, gated, scale, low)

    def column_copy(slot, peer):
        return remote(low.at[peer], columns.at[d], column_sem, slot, dp=peer)

    def column_arrival(slot, peer):
        return remote(low.at[peer], columns.at[peer], column_sem, slot, dp=peer)

    peers = (across, diagonal, beside)
    for slot, peer in enumerate(peers):
        column_copy(slot, peer).start()
    columns[d] = low[d]
    with jax.named_scope("partial_wait"):
        for slot in (1, 2, 3):
            partial_copy(slot, arrival=True).wait_recv()

    with jax.named_scope("gate"):
        gate_phase(
            act, cum_wide, inside, skip_wide, gate, norm_weight, gated, scale, query_t,
            d // 2, normed_sent, normed_grad, scanned_grad, gate_grad, norm_grad, skip_sum,
            back_states,
            lambda number: pair_copy(back_states, back_other, back_sem, number).start(),
        )

    store_gate = pltpu.make_async_copy(gate_grad, gate_out, local_sem.at[0])
    store_gate.start()

    def plan_for(order):
        size, base, offset = own_rows, 0, 0
        plan = []
        for bit in order:
            mine = q // bit % 2
            halves = size // 2 % 16 == 0
            if halves:
                size = size // 2
                keep, give = base + mine * size, base + (1 - mine) * size
                base = keep
            else:
                keep, give = base, base
            plan.append((bit, halves, size, keep, give, offset))
            offset = offset + size
        return plan

    plans = (plan_for(bits), plan_for(bits[1:] + bits[:1]))
    levels = len(bits)
    halvings = [number for number in range(levels) if plans[0][number][1]]
    half_width = cotangent.shape[1] // 2

    def rows_at(start, length):
        return pl.ds(pl.multiple_of(start, 16), length)

    def lanes_of(part):
        return pl.ds(part * half_width, half_width)

    def share_copy(number, part):
        bit, _, length, _, _, place = plans[part][number]
        rows = pl.ds(place, length)
        return remote(
            weight_out.at[part, rows], weight_in.at[part, rows],
            share_sem, 2 * number + part, seq=toggled(q, bit),
        )

    def share_start(number, part):
        _, _, length, _, give, place = plans[part][number]
        weight_out[part, place : place + length] = weight_grad[
            rows_at(give, length), lanes_of(part)
        ].astype(BF16)
        share_copy(number, part).start()

    def share_finish(number, part):
        _, halves, length, keep, _, place = plans[part][number]
        with jax.named_scope("share_wait"):
            share_copy(number, part).wait()
        found = weight_in[part, place : place + length].astype(F32)
        if halves:
            kept = weight_grad[rows_at(keep, length), lanes_of(part)]
        else:
            kept = weight_out[part, place : place + length].astype(F32)
        weight_grad[rows_at(keep, length), lanes_of(part)] = kept + found

    def spread_copy(number, part, arrival=False):
        bit, _, length, keep, give, _ = plans[part][number]
        place = weight_all.at[rows_at(give if arrival else keep, length), lanes_of(part)]
        return remote(
            place, place, share_sem, 2 * (levels + number) + part, seq=toggled(q, bit)
        )

    def weight_event(stage, part):
        if stage < levels:
            share_finish(stage - 1, part)
            share_start(stage, part)
        elif stage == levels:
            share_finish(stage - 1, part)
            _, _, length, keep, _, _ = plans[part][-1]
            rows = rows_at(keep, length)
            weight_all[rows, lanes_of(part)] = weight_grad[rows, lanes_of(part)].astype(BF16)
            spread_copy(halvings[-1], part).start()
        else:
            number = halvings[levels - stage]
            with jax.named_scope("spread_wait"):
                spread_copy(number, part, arrival=True).wait_recv()
            if number > 0:
                spread_copy(number - 1, part).start()

    events = [(stage, 1 - part) for stage in range(1, levels + len(halvings) + 1) for part in range(2)]
    distance = groups_along - 1 - group
    far = distance >= 2
    ready_at = jnp.where(distance == 1, messages // 2, messages - 1)

    def weights_ready():
        for slot, peer in enumerate(peers):
            with jax.named_scope("column_wait"):
                column_arrival(slot, peer).wait_recv()
        with jax.named_scope("weight_dot"):
            weight_phase(columns, cotangents, weight_grad)
        share_start(0, 1)
        share_start(0, 0)

    def back_before(number):
        pl.when((number == 0) & far)(weights_ready)

    def back_step(number):
        chain_step(
            number, back_states, back_other, end_grad, back_sems,
            jnp.logical_not(odd), ends, begins, q - 2,
        )
        pl.when((number == ready_at) & jnp.logical_not(far))(weights_ready)
        for place, event in zip(CHAIN_HOOKS, events):
            pl.when((number == place) & far)(functools.partial(weight_event, *event))

    with jax.named_scope("inside_grad"):
        inside_grad_phase(
            act, cum_wide, dt_wide, cum_rows, scores, inside, scanned_grad, entering,
            scaled_grad, score_grad, query_grad, row_sums, back_before, back_step,
        )
    near = jnp.logical_not(far)

    def end_before(number):
        return_copy(back_other, end_grad, back_sems[2], number, arrival=True).wait_recv()

    def end_hook(index):
        for number in range(2):
            pl.when((index == NEAR_HOOKS[number]) & near)(
                functools.partial(weight_event, *events[number])
            )
            pl.when((index == FAR_HOOKS[number]) & far)(
                functools.partial(weight_event, *events[number + 2])
            )

    with jax.named_scope("end"):
        end_phase(
            act, slope, cum_wide, dt_wide, cum_cols, dt_cols, decay_wide, skip_wide, scanned_grad,
            scaled_grad, score_grad, query_grad, row_sums, entering, end_grad, key_grad, skip_sum,
            step, step_bias, decay_log, raw, halo, taps, window, filtered_grad,
            step_grad, filter_sums, head_sums, end_before, end_hook,
        )
    left = events[4:]
    heads_out[...] = filtered_grad[0:8, :]
    back_copy = remote(heads_out, following, halo_sem, 1, seq=q - 1)
    pl.when(jnp.logical_not(first))(back_copy.start)

    @pl.when(last)
    def _():
        following[...] = jnp.zeros_like(following)

    small[...] = filter_sums[...]
    small[count + 1 : count + 2, 0:inner] = norm_grad[0:1, :]
    for row in range(3):
        small[count + 2 : count + 3, row * LANES : (row + 1) * LANES] = head_sums[row : row + 1, :]

    steps = [("dp", bit) for bit in (1, 2)] + [("seq", bit) for bit in bits]

    def small_copy(number):
        axis, bit = steps[number]
        target = {"seq": toggled(q, bit)} if axis == "seq" else {"dp": toggled(d, bit)}
        return remote(small_in.at[2 * number], small_in.at[2 * number + 1], small_sem, number, **target)

    def small_start(number):
        small_in[2 * number] = small[...]
        small_copy(number).start()

    def small_step(number):
        with jax.named_scope("small_wait"):
            small_copy(number).wait()
        small[...] += small_in[2 * number + 1]
        if number + 1 < len(steps):
            small_start(number + 1)

    small_start(0)

    @pl.when(near)
    def _():
        weight_event(*events[2])
        weight_event(*events[3])

    small_step(0)
    pl.when(jnp.logical_not(last))(back_copy.wait_recv)
    with jax.named_scope("filter_grad"):
        filter_grad_phase(filtered_grad, following, taps, window, input_grad)
    number = 1
    while left or number < len(steps):
        for event in left[:2]:
            weight_event(*event)
        left = left[2:]
        if number < len(steps):
            small_step(number)
            number += 1

    store_weight = pltpu.make_async_copy(weight_all, weight_result, local_sem.at[1])
    store_weight.start()
    filter_out[...] = small[0 : count + 1, :]
    for index in range(inner // LANES):
        norm_out[index : index + 1, :] = small[
            count + 1 : count + 2, index * LANES : (index + 1) * LANES
        ]
    for row in range(3):
        head_out[row : row + 1, :] = small[
            count + 2 : count + 3, row * LANES : row * LANES + step.shape[0]
        ]
    for number in halvings:
        for part in range(2):
            spread_copy(number, part).wait_send()
    gather(d, 0, across).wait_send()
    gather(d, 1, beside).wait_send()
    gather(across, 2, beside).wait_send()
    for slot in (1, 2, 3):
        partial_copy(slot).wait_send()
    for slot, peer in enumerate(peers):
        column_copy(slot, peer).wait_send()
    pl.when(jnp.logical_not(last))(halo_copy.wait_send)
    pl.when(jnp.logical_not(first))(back_copy.wait_send)

    def drain(index, carry):
        chain_end(index, states, states_other, entering, ahead_sems, ends, q + 2)
        chain_end(index, back_states, back_other, end_grad, back_sems, begins, q - 2)
        return carry

    with jax.named_scope("drain"):
        lax.fori_loop(0, messages, drain, 0)
    store_gate.wait()
    store_weight.wait()


def body(
    conv_input,
    gate_input,
    step_input,
    filter_taps,
    filter_bias,
    step_bias,
    decay_log,
    skip_gain,
    norm_weight,
    output_weight,
    output_grad,
):
    raw, gate, step, cotangent = conv_input[0], gate_input[0], step_input[0], output_grad[0]
    tokens, channels = raw.shape
    inner = gate.shape[1]
    heads = step.shape[0]
    own_rows, width = output_weight.shape
    count = filter_taps.shape[0]
    spans, groups = lax.axis_size("seq"), lax.axis_size("dp")
    half = tokens // 2
    chunks = inner // LANES
    messages = chunks // 2
    assert groups == 4 and tokens % 256 == 0 and inner % (2 * LANES) == 0
    levels = spans.bit_length() - 1
    shared, size = 0, own_rows
    for _ in range(levels):
        size = size // 2 if size // 2 % 16 == 0 else size
        shared += size
    wide = pltpu.VMEM((tokens, inner), F32)
    full = pltpu.VMEM((tokens, channels), F32)
    columns = pltpu.VMEM((tokens, LANES), F32)
    row8 = pltpu.VMEM((8, inner), F32)
    stored = pltpu.VMEM((chunks, LANES, LANES), F32)
    turned = pltpu.VMEM((2, LANES, tokens), BF16)
    squares = pltpu.VMEM((3, half, half), F32)
    edge = pltpu.VMEM((8, channels), F32)
    sems = pltpu.SemaphoreType.DMA
    scratch = [
        pltpu.VMEM((tokens, inner), BF16), pltpu.VMEM((tokens, inner), BF16),
        pltpu.VMEM((own_rows, width), F32), edge, row8,
        pltpu.VMEM((16, channels), BF16),
        pltpu.VMEM((own_rows, width), BF16),
        pltpu.VMEM((groups, tokens, width), BF16),
        full, full, wide, wide, row8, row8,
        pltpu.VMEM((heads, 1, tokens), F32), columns, columns, turned, turned,
        pltpu.VMEM((2, tokens + 8, LANES), F32), squares,
        stored, stored, stored, wide, wide, columns,
        pltpu.VMEM((groups, tokens, own_rows), BF16),
        pltpu.VMEM((groups, tokens, own_rows), BF16),
        pltpu.VMEM((groups, tokens, own_rows), F32),
        pltpu.VMEM((groups, tokens, own_rows), BF16),
        pltpu.VMEM((tokens, own_rows), F32),
        pltpu.VMEM((2, tokens, own_rows), BF16),
        wide, wide, row8, row8,
        stored, stored, stored, squares, columns, columns, columns,
        edge, pltpu.VMEM((8, LANES), F32), edge, edge,
        pltpu.VMEM((2, shared, width // 2), BF16),
        pltpu.VMEM((2, shared, width // 2), BF16),
        pltpu.VMEM((own_rows, width), BF16),
        pltpu.VMEM((2 * (levels + 2), 8, channels), F32),
        sems((3,)), sems((2, 2)), sems((2, 1)), sems((2, 3)), sems((2, 3)), sems((2, 3)),
        sems((2, messages)), sems((2, messages)), sems((2, 2, messages)), sems((2, 2, messages)),
        sems((2, 4 * levels)), sems((2, levels + 2)),
    ]
    outs = [
        ((tokens, channels), BF16), ((tokens, inner), BF16), ((heads, tokens), F32),
        ((own_rows, width), BF16), ((count + 1, channels), F32), ((chunks, LANES), F32),
        ((3, heads), F32),
    ]
    args = (
        raw, step, filter_taps, filter_bias.reshape(channels // LANES, LANES),
        step_bias[None], decay_log[None], skip_gain[None],
        norm_weight.reshape(chunks, LANES), output_weight, cotangent, gate,
    )
    vmem = pl.BlockSpec(memory_space=pltpu.VMEM)
    anywhere = pl.BlockSpec(memory_space=pl.ANY)
    results = pl.pallas_call(
        functools.partial(layer_kernel, spans, groups),
        out_shape=[jax.ShapeDtypeStruct(shape, kind) for shape, kind in outs],
        in_specs=[vmem] * (len(args) - 3) + [anywhere] * 3,
        out_specs=[vmem, anywhere, vmem, anywhere, vmem, vmem, vmem],
        scratch_shapes=scratch,
        compiler_params=pltpu.CompilerParams(
            vmem_limit_bytes=67043328, has_side_effects=True, collective_id=0
        ),
    )(*args)
    kinds = [outs[number] for number in range(len(outs))]
    kinds[3] = ((own_rows, width), F32)
    input_grad, gate_grad, step_grad, weight_grad, filter_grads, norm_grad, head_grads = pl.pallas_call(
        finish_kernel,
        out_shape=[jax.ShapeDtypeStruct(shape, kind) for shape, kind in kinds],
        in_specs=[anywhere] * len(outs),
        out_specs=[anywhere] * len(outs),
        scratch_shapes=[pltpu.VMEM(*out) for out in outs]
        + [pltpu.VMEM(*kinds[3]), sems((len(outs),)), sems((len(outs),))],
        compiler_params=pltpu.CompilerParams(vmem_limit_bytes=67043328),
    )(*results)
    return (
        input_grad[None], gate_grad[None], step_grad[None], weight_grad,
        filter_grads, norm_grad.reshape(inner), head_grads,
    )


def finish_kernel(*refs):
    count = (len(refs) - 3) // 3
    sources, targets, held = refs[:count], refs[count : 2 * count], list(refs[2 * count : 3 * count])
    widened, load_sem, store_sem = refs[3 * count :]
    loads = [
        pltpu.make_async_copy(source, buffer, load_sem.at[number])
        for number, (source, buffer) in enumerate(zip(sources, held))
    ]
    order = [3] + [number for number in range(count) if number != 3]
    for number in order:
        loads[number].start()
    stores = []
    for number in order:
        loads[number].wait()
        buffer = held[number]
        if number == 3:
            widened[...] = buffer[...].astype(F32)
            buffer = widened
        store = pltpu.make_async_copy(buffer, targets[number], store_sem.at[number])
        store.start()
        stores.append(store)
    for store in stores:
        store.wait()


def solution(mesh):
    return jax.shard_map(
        body,
        mesh=mesh,
        in_specs=(
            P("dp", "seq", None),
            P("dp", "seq", None),
            P("dp", None, "seq"),
            P(),
            P(),
            P(),
            P(),
            P(),
            P(),
            P("dp", None),
            P("dp", "seq", None),
        ),
        out_specs=(
            P("dp", "seq", None),
            P("dp", "seq", None),
            P("dp", None, "seq"),
            P("dp", None),
            P(),
            P(),
            P(),
        ),
        check_vma=False,
    )
```

time: 211 us -> 140 us (0.66)
  Pallas kernels: 192 us -> 138 us
  local copies, waits for them, and re-layouts: 17.5 us -> 0 us
    pallas_call x1, Pallas kernels: 192 us -> 134 us  [body(): pl.pallas_call(functools.partial(layer_kernel, spans, groups), out_shape=...]
    broadcast_in_dim x6 -> x0, local copies, waits for them, and re-layouts: 7.2 us -> none  [the longest x1 1.34 us: body(): step_bias[:, None]]
    unnamed x13 -> x0, local copies, waits for them, and re-layouts: 6.74 us -> none
    pallas_call x0 -> x1, Pallas kernels: none -> 4.38 us  [body(): pl.pallas_call(finish_kernel, out_shape=[jax.ShapeDtypeStruct(shape, kind...]
    slice x2 -> x0, local copies, waits for them, and re-layouts: 2.92 us -> none  [the longest x1 1.62 us: body(): small[count + 1, :inner]]
where the time goes in v2:
time: 140 us; the launch traced here: 139 us
  Pallas kernels  138 us (99%)
    pallas_call x1, Pallas kernels, body(): pl.pallas_call(functools.partial(layer_kernel, spans, groups), out_shape=...  134 us
    pallas_call x1, Pallas kernels, body(): pl.pallas_call(finish_kernel, out_shape=[jax.ShapeDtypeStruct(shape, kind...  4.38 us

profile of v2, /device:TPU:0, one launch (start us, length us, event | category | flops | bytes accessed | tf_op | source)
XLA Modules:
  0.0 138.7 jit_solution(17936329912750438335)
XLA Ops:
  0.6 133.7 %shard_map.162 = (bf16[256,2816]{1,0:T(8,128)(2,1)}, bf16[256,2560]{1,0:T(8,128)(2,1)}, f32[40,256]{1,0:T(8,128)}, bf16[640,1280]{1,0:T(8,128)(2,1)}, f32[5,2816...) custom-call(bf16[256,2816]{1,0:T(8,128)(2,1)} %bitcast.13, f32[40,256]{1,0:T(8,128)} %bitcast.16, f32[4,2816]{1,0:T(4,128)} %taps.1, ...), custom_call_target="tpu_custom_call" | custom-call | tf_op jit(solution)/shard_map/pallas_call | solution.py:1039
  134.4 4.4 %shard_map.163 = (bf16[256,2816]{1,0:T(8,128)(2,1)}, bf16[256,2560]{1,0:T(8,128)(2,1)}, f32[40,256]{1,0:T(8,128)}, f32[640,1280]{1,0:T(8,128)}, f32[5,2816]{1,0:...) custom-call(bf16[256,2816]{1,0:T(8,128)(2,1)} %get-tuple-element.21.refs_0_, bf16[256,2560]{1,0:T(8,128)(2,1)} %get-tuple-element.22.refs_1_, ...), custom_call_target="tpu_custom_call" | custom-call | tf_op jit(solution)/shard_map/pallas_call | solution.py:1051

commit v3 on v2

--- a/solution.py
+++ b/solution.py
@@ -14,9 +14,9 @@
 LANES = 128
 HEAD_DIM = 64
 MESH = pl.DeviceIdType.MESH
-CHAIN_HOOKS = (6, 9)
-FAR_HOOKS = (4, 8)
-NEAR_HOOKS = (6, 9)
+CHAIN_HOOKS = (6, 6, 9, 9)
+FAR_HOOKS = (4, 4, 8, 8)
+NEAR_HOOKS = (6, 6, 9, 9)
 NN = (((1,), (0,)), ((), ()))
 NT = (((1,), (1,)), ((), ()))
 TN = (((0,), (0,)), ((), ()))
@@ -675,34 +675,33 @@
         gather(across, 0, across).wait_recv()
         gather(across, 2, beside).start()
 
+    def partial_slots(first, last):
+        def each(at, carry):
+            partial_chunk(at)
+            return carry
+
+        lax.fori_loop(first * per_slot, last * per_slot, each, 0)
+
     def ahead_before(number):
         @pl.when((number == 0) & jnp.logical_not(early))
         def _():
             gather(beside, 1, beside).wait_recv()
-
-            def several(first, last):
-                def each(at, carry):
-                    partial_chunk(at)
-                    return carry
-
-                lax.fori_loop(first * per_slot, last * per_slot, each, 0)
-
-            several(0, 2)
+            partial_slots(0, 2)
             across_arrives()
-            several(2, 3)
+            partial_slots(2, 3)
             gather(diagonal, 2, beside).wait_recv()
-            several(3, 4)
+            partial_slots(3, 4)
 
     def ahead_step(number):
         chain_step(
             number, states, states_other, entering, ahead_sems, odd, begins, ends, q + 2
         )
 
-        @pl.when(early)
+        pl.when(early & (number == per_slot))(across_arrives)
+        pl.when(early & (number == per_slot + per_slot // 2))(gather(diagonal, 2, beside).wait_recv)
+
+        @pl.when(early & (number >= per_slot))
         def _():
-            pl.when(number == per_slot // 2)(gather(beside, 1, beside).wait_recv)
-            pl.when(number == per_slot)(across_arrives)
-            pl.when(number == per_slot + per_slot // 2)(gather(diagonal, 2, beside).wait_recv)
             for j in range(2):
                 partial_chunk(2 * number + j)
 
@@ -710,6 +709,11 @@
         inside_phase(
             act, cum_wide, dt_wide, cum_rows, scores, inside, ahead_before, ahead_step,
         )
+
+    @pl.when(early)
+    def _():
+        gather(beside, 1, beside).wait_recv()
+        partial_slots(0, 2)
 
     with jax.named_scope("return_wait"):
         for number in range(messages):
@@ -759,28 +763,31 @@
             offset = offset + size
         return plan
 
-    plans = (plan_for(bits), plan_for(bits[1:] + bits[:1]))
+    plans = (plan_for(bits), plan_for(bits[1:] + bits[:1])) * 2
     levels = len(bits)
     halvings = [number for number in range(levels) if plans[0][number][1]]
-    half_width = cotangent.shape[1] // 2
+    tiles = cotangent.shape[1] // LANES
+    parts = 4
+    edges = [-(-tiles * part // parts) * LANES for part in range(parts + 1)]
+    order = (1, 3, 0, 2)
 
     def rows_at(start, length):
         return pl.ds(pl.multiple_of(start, 16), length)
 
     def lanes_of(part):
-        return pl.ds(part * half_width, half_width)
+        return pl.ds(edges[part], edges[part + 1] - edges[part])
 
     def share_copy(number, part):
         bit, _, length, _, _, place = plans[part][number]
         rows = pl.ds(place, length)
         return remote(
-            weight_out.at[part, rows], weight_in.at[part, rows],
-            share_sem, 2 * number + part, seq=toggled(q, bit),
+            weight_out.at[rows, lanes_of(part)], weight_in.at[rows, lanes_of(part)],
+            share_sem, 4 * number + part, seq=toggled(q, bit),
         )
 
     def share_start(number, part):
         _, _, length, _, give, place = plans[part][number]
-        weight_out[part, place : place + length] = weight_grad[
+        weight_out[place : place + length, lanes_of(part)] = weight_grad[
             rows_at(give, length), lanes_of(part)
         ].astype(BF16)
         share_copy(number, part).start()
@@ -789,18 +796,18 @@
         _, halves, length, keep, _, place = plans[part][number]
         with jax.named_scope("share_wait"):
             share_copy(number, part).wait()
-        found = weight_in[part, place : place + length].astype(F32)
+        found = weight_in[place : place + length, lanes_of(part)].astype(F32)
         if halves:
             kept = weight_grad[rows_at(keep, length), lanes_of(part)]
         else:
-            kept = weight_out[part, place : place + length].astype(F32)
+            kept = weight_out[place : place + length, lanes_of(part)].astype(F32)
         weight_grad[rows_at(keep, length), lanes_of(part)] = kept + found
 
     def spread_copy(number, part, arrival=False):
         bit, _, length, keep, give, _ = plans[part][number]
         place = weight_all.at[rows_at(give if arrival else keep, length), lanes_of(part)]
         return remote(
-            place, place, share_sem, 2 * (levels + number) + part, seq=toggled(q, bit)
+            place, place, share_sem, 4 * (levels + number) + part, seq=toggled(q, bit)
         )
 
     def weight_event(stage, part):
@@ -820,7 +827,7 @@
             if number > 0:
                 spread_copy(number - 1, part).start()
 
-    events = [(stage, 1 - part) for stage in range(1, levels + len(halvings) + 1) for part in range(2)]
+    events = [(stage, part) for stage in range(1, levels + len(halvings) + 1) for part in order]
     distance = groups_along - 1 - group
     far = distance >= 2
     ready_at = jnp.where(distance == 1, messages // 2, messages - 1)
@@ -831,8 +838,8 @@
                 column_arrival(slot, peer).wait_recv()
         with jax.named_scope("weight_dot"):
             weight_phase(columns, cotangents, weight_grad)
-        share_start(0, 1)
-        share_start(0, 0)
+        for part in order:
+            share_start(0, part)
 
     def back_before(number):
         pl.when((number == 0) & far)(weights_ready)
@@ -857,12 +864,12 @@
         return_copy(back_other, end_grad, back_sems[2], number, arrival=True).wait_recv()
 
     def end_hook(index):
-        for number in range(2):
+        for number in range(parts):
             pl.when((index == NEAR_HOOKS[number]) & near)(
                 functools.partial(weight_event, *events[number])
             )
             pl.when((index == FAR_HOOKS[number]) & far)(
-                functools.partial(weight_event, *events[number + 2])
+                functools.partial(weight_event, *events[number + parts])
             )
 
     with jax.named_scope("end"):
@@ -872,7 +879,7 @@
             step, step_bias, decay_log, raw, halo, taps, window, filtered_grad,
             step_grad, filter_sums, head_sums, end_before, end_hook,
         )
-    left = events[4:]
+    left = events[2 * parts :]
     heads_out[...] = filtered_grad[0:8, :]
     back_copy = remote(heads_out, following, halo_sem, 1, seq=q - 1)
     pl.when(jnp.logical_not(first))(back_copy.start)
@@ -908,21 +915,26 @@
 
     @pl.when(near)
     def _():
-        weight_event(*events[2])
-        weight_event(*events[3])
-
+        for event in events[parts : 2 * parts]:
+            weight_event(*event)
+
+    for event in left[:parts]:
+        weight_event(*event)
+    left = left[parts:]
     small_step(0)
     pl.when(jnp.logical_not(last))(back_copy.wait_recv)
     with jax.named_scope("filter_grad"):
         filter_grad_phase(filtered_grad, following, taps, window, input_grad)
-    number = 1
+    small_step(1)
+    number = 2
     while left or number < len(steps):
-        for event in left[:2]:
+        for event in left[:parts]:
             weight_event(*event)
-        left = left[2:]
-        if number < len(steps):
-            small_step(number)
-            number += 1
+        left = left[parts:]
+        for _ in range(2 if len(left) == parts else 1):
+            if number < len(steps):
+                small_step(number)
+                number += 1
 
     store_weight = pltpu.make_async_copy(weight_all, weight_result, local_sem.at[1])
     store_weight.start()
@@ -936,7 +948,7 @@
             count + 2 : count + 3, row * LANES : row * LANES + step.shape[0]
         ]
     for number in halvings:
-        for part in range(2):
+        for part in range(parts):
             spread_copy(number, part).wait_send()
     gather(d, 0, across).wait_send()
     gather(d, 1, beside).wait_send()
@@ -1016,13 +1028,13 @@
         wide, wide, row8, row8,
         stored, stored, stored, squares, columns, columns, columns,
         edge, pltpu.VMEM((8, LANES), F32), edge, edge,
-        pltpu.VMEM((2, shared, width // 2), BF16),
-        pltpu.VMEM((2, shared, width // 2), BF16),
+        pltpu.VMEM((shared, width), BF16),
+        pltpu.VMEM((shared, width), BF16),
         pltpu.VMEM((own_rows, width), BF16),
         pltpu.VMEM((2 * (levels + 2), 8, channels), F32),
         sems((3,)), sems((2, 2)), sems((2, 1)), sems((2, 3)), sems((2, 3)), sems((2, 3)),
         sems((2, messages)), sems((2, messages)), sems((2, 2, messages)), sems((2, 2, messages)),
-        sems((2, 4 * levels)), sems((2, levels + 2)),
+        sems((2, 8 * levels)), sems((2, levels + 2)),
     ]
     outs = [
         ((tokens, channels), BF16), ((tokens, inner), BF16), ((heads, tokens), F32),

time: 140 us -> 136 us (0.971)
  Pallas kernels: 138 us -> 135 us
    pallas_call x1, Pallas kernels: 134 us -> 131 us  [body(): pl.pallas_call(functools.partial(layer_kernel, spans, groups), out_shape=...]
where the time goes in v3:
time: 136 us
  Pallas kernels  135 us (99%)
    pallas_call x1, Pallas kernels, body(): pl.pallas_call(functools.partial(layer_kernel, spans, groups), out_shape=...  131 us
    pallas_call x1, Pallas kernels, body(): pl.pallas_call(finish_kernel, out_shape=[jax.ShapeDtypeStruct(shape, kind...  4.38 us

profile of v3, /device:TPU:0, one launch (start us, length us, event | category | flops | bytes accessed | tf_op | source)
XLA Modules:
  0.0 136.0 jit_solution(2495911286419743344)
XLA Ops:
  0.6 130.9 %shard_map.162 = (bf16[256,2816]{1,0:T(8,128)(2,1)}, bf16[256,2560]{1,0:T(8,128)(2,1)}, f32[40,256]{1,0:T(8,128)}, bf16[640,1280]{1,0:T(8,128)(2,1)}, f32[5,2816...) custom-call(bf16[256,2816]{1,0:T(8,128)(2,1)} %bitcast.13, f32[40,256]{1,0:T(8,128)} %bitcast.16, f32[4,2816]{1,0:T(4,128)} %taps.1, ...), custom_call_target="tpu_custom_call" | custom-call | tf_op jit(solution)/shard_map/pallas_call | solution.py:1051
  131.6 4.4 %shard_map.163 = (bf16[256,2816]{1,0:T(8,128)(2,1)}, bf16[256,2560]{1,0:T(8,128)(2,1)}, f32[40,256]{1,0:T(8,128)}, f32[640,1280]{1,0:T(8,128)}, f32[5,2816]{1,0:...) custom-call(bf16[256,2816]{1,0:T(8,128)(2,1)} %get-tuple-element.21.refs_0_, bf16[256,2560]{1,0:T(8,128)(2,1)} %get-tuple-element.22.refs_1_, ...), custom_call_target="tpu_custom_call" | custom-call | tf_op jit(solution)/shard_map/pallas_call | solution.py:1063

commit v4 on v3

--- a/solution.py
+++ b/solution.py
@@ -918,14 +918,14 @@
         for event in events[parts : 2 * parts]:
             weight_event(*event)
 
-    for event in left[:parts]:
-        weight_event(*event)
-    left = left[parts:]
     small_step(0)
     pl.when(jnp.logical_not(last))(back_copy.wait_recv)
     with jax.named_scope("filter_grad"):
         filter_grad_phase(filtered_grad, following, taps, window, input_grad)
     small_step(1)
+    for event in left[:parts]:
+        weight_event(*event)
+    left = left[parts:]
     number = 2
     while left or number < len(steps):
         for event in left[:parts]:

time: 136 us -> 137 us (level)
  no operation moved by 1% of the time
where the time goes in v4:
time: 137 us; the launch traced here: 136 us
  Pallas kernels  136 us (99%)
    pallas_call x1, Pallas kernels, body(): pl.pallas_call(functools.partial(layer_kernel, spans, groups), out_shape=...  131 us
    pallas_call x1, Pallas kernels, body(): pl.pallas_call(finish_kernel, out_shape=[jax.ShapeDtypeStruct(shape, kind...  4.38 us

profile of v4, /device:TPU:0, one launch (start us, length us, event | category | flops | bytes accessed | tf_op | source)
XLA Modules:
  0.0 136.5 jit_solution(1316900271433266908)
XLA Ops:
  0.6 131.4 %shard_map.162 = (bf16[256,2816]{1,0:T(8,128)(2,1)}, bf16[256,2560]{1,0:T(8,128)(2,1)}, f32[40,256]{1,0:T(8,128)}, bf16[640,1280]{1,0:T(8,128)(2,1)}, f32[5,2816...) custom-call(bf16[256,2816]{1,0:T(8,128)(2,1)} %bitcast.13, f32[40,256]{1,0:T(8,128)} %bitcast.16, f32[4,2816]{1,0:T(4,128)} %taps.1, ...), custom_call_target="tpu_custom_call" | custom-call | tf_op jit(solution)/shard_map/pallas_call | solution.py:1051
  132.1 4.4 %shard_map.163 = (bf16[256,2816]{1,0:T(8,128)(2,1)}, bf16[256,2560]{1,0:T(8,128)(2,1)}, f32[40,256]{1,0:T(8,128)}, f32[640,1280]{1,0:T(8,128)}, f32[5,2816]{1,0:...) custom-call(bf16[256,2816]{1,0:T(8,128)(2,1)} %get-tuple-element.21.refs_0_, bf16[256,2560]{1,0:T(8,128)(2,1)} %get-tuple-element.22.refs_1_, ...), custom_call_target="tpu_custom_call" | custom-call | tf_op jit(solution)/shard_map/pallas_call | solution.py:1063
